TPU v7x, 32 devices: a whole 2x2x4 slice. The times are simulated.
32 devices in a mesh: rep: 2 (over x), tp: 4 (over z), dp: 4 (over y, core).
Axes of the slice: x: 2, y: 2, z: 4, core: 2. Of those that a mesh axis runs over, the one named last changes fastest.
Arguments:
- x: bfloat16 [256, 2048], P(('rep', 'dp')), parts along dimension 0
- lengths: int32 [256], P(('rep', 'dp')), parts along dimension 0
- cache0: bfloat16 [256, 256, 576], P(('rep', 'dp')), parts along dimension 0
- cache1: bfloat16 [256, 256, 576], P(('rep', 'dp')), parts along dimension 0
- attn_gain: float32 [2, 2048], replicated
- kv_gain: float32 [2, 512], replicated
- q_gain: float32 [2, 1536], replicated
- ffn_gain: float32 [2, 2048], replicated
- w_dkv: bfloat16 [2, 2048, 576], replicated
- w_qa: bfloat16 [2, 2048, 1536], replicated
- w_qb: bfloat16 [2, 1536, 3072], P(None, None, 'tp')
- w_uk: bfloat16 [2, 16, 128, 512], P(None, 'tp')
- w_uv: bfloat16 [2, 16, 512, 128], P(None, 'tp')
- w_o: bfloat16 [2, 2048, 2048], P(None, 'tp')
- w_gate: bfloat16 [2, 2048, 11264], replicated
- w_up: bfloat16 [2, 2048, 11264], replicated
- w_down: bfloat16 [2, 11264, 2048], replicated
Outputs:
- output 1: bfloat16 [256, 2048], P(('rep', 'dp')), parts along dimension 0
- output 2: bfloat16 [256, 256, 576], P(('rep', 'dp')), parts along dimension 0
- output 3: bfloat16 [256, 256, 576], P(('rep', 'dp')), parts along dimension 0
There are 2 independent parts. A program takes and returns all parts, laid end to end along the dimension named above; an argument that names none is the same for every part.
All inputs are finite; a program needn't handle non-finite values.
Results may differ from a plain program's by a relative error of at most 0.0148903.
Values are sent between devices in bfloat16 or wider.
A program may use at most 1.5 GiB of HBM per device.

v0:
```python
import jax
import jax.numpy as jnp
from jax import lax
from jax.sharding import PartitionSpec as P

NORM_EPS = 1e-6
ROPE_BASE = 10000.0


def rms_norm(values, gain_vec):
    wide_vals = values.astype(jnp.float32)
    inv_rms = lax.rsqrt(jnp.mean(wide_vals * wide_vals, axis=-1, keepdims=True) + NORM_EPS)
    return (wide_vals * inv_rms * gain_vec).astype(jnp.bfloat16)


def rope_tables(lengths, rope_dim):
    half_dim = rope_dim // 2
    inv_freq = ROPE_BASE ** (-2.0 * jnp.arange(half_dim).astype(jnp.float32) / rope_dim)
    angles = lengths.astype(jnp.float32)[:, None] * inv_freq[None, :]
    return jnp.cos(angles), jnp.sin(angles)


def rotate(values, cos_tab, sin_tab):
    half_dim = values.shape[-1] // 2
    first_half = values[..., :half_dim]
    second_half = values[..., half_dim:]
    return jnp.concatenate([first_half * cos_tab - second_half * sin_tab, second_half * cos_tab + first_half * sin_tab], axis=-1)


def attention_local(x_rows, lengths, cache, cos_tab, sin_tab, attn_g, kv_g, q_g, w_dkv, w_qa, w_qb, w_uk, w_uv, w_o):
    row_count = x_rows.shape[0]
    head_count, nope_dim, value_a7 = w_uk.shape
    qk_width = w_qb.shape[1] // head_count
    slot_ids = jnp.arange(cache.shape[1])
    normed = rms_norm(x_rows, attn_g)
    kv_lat = jnp.dot(normed, w_dkv, preferred_element_type=jnp.float32)
    new_entry = jnp.concatenate([rms_norm(kv_lat[:, :value_a7], kv_g), rotate(kv_lat[:, value_a7:], cos_tab, sin_tab).astype(jnp.bfloat16)], axis=-1)
    is_slot = (slot_ids[None, :] == lengths[:, None])[:, :, None]
    new_cache = jnp.where(is_slot, new_entry[:, None, :], cache)
    q_low = rms_norm(jnp.dot(normed, w_qa, preferred_element_type=jnp.float32), q_g)
    q_full = jnp.dot(q_low, w_qb, preferred_element_type=jnp.float32).reshape(row_count, head_count, qk_width)
    q_nope = q_full[:, :, :nope_dim].astype(jnp.bfloat16)
    q_rot = rotate(q_full[:, :, nope_dim:], cos_tab[:, None, :], sin_tab[:, None, :]).astype(jnp.bfloat16)
    q_lat = jnp.einsum('bhn,hnk->bhk', q_nope, w_uk, preferred_element_type=jnp.float32).astype(jnp.bfloat16)
    query_vec = jnp.concatenate([q_lat, q_rot], axis=-1)
    scores = jnp.einsum('bhk,btk->bht', query_vec, new_cache, preferred_element_type=jnp.float32) * qk_width ** -0.5
    valid_mask = (slot_ids[None, :] <= lengths[:, None])[:, None, :]
    att_probs = jax.nn.softmax(jnp.where(valid_mask, scores, -1e30), axis=-1).astype(jnp.bfloat16)
    lat_out = jnp.einsum('bht,btk->bhk', att_probs, new_cache, preferred_element_type=jnp.float32)[:, :, :value_a7].astype(jnp.bfloat16)
    head_out = jnp.einsum('cil,ilw->ciw', lat_out, w_uv, preferred_element_type=jnp.float32).astype(jnp.bfloat16)
    attn_part = jnp.dot(head_out.reshape(row_count, head_count * w_uv.shape[2]), w_o, preferred_element_type=jnp.float32)
    return attn_part, new_cache


def solution(mesh):
    tp_size = mesh.shape['tp']
    dp_size = mesh.shape['dp']
    row_spec = P(('rep', 'dp'), None)
    cache_spec = P(('rep', 'dp'), None, None)
    in_specs = (row_spec, P(('rep', 'dp')), cache_spec, cache_spec, P(), P(), P(), P(), P(), P(), P(None, None, 'tp'), P(None, 'tp', None, None), P(None, 'tp', None, None), P(None, 'tp', None), P(), P(), P())
    out_specs = (row_spec, cache_spec, cache_spec)

    def local_step(x, lengths, cache0, cache1, attn_gain, kv_gain, q_gain, ffn_gain, w_dkv, w_qa, w_qb, w_uk, w_uv, w_o, w_gate, w_up, w_down):
        row_count, model_dim = x.shape
        ffn_width = w_gate.shape[2] // (tp_size * dp_size)
        ffn_start = (lax.axis_index('tp') * dp_size + lax.axis_index('dp')) * ffn_width
        rope_dim = cache0.shape[2] - w_uk.shape[3]
        cos_tab, sin_tab = rope_tables(lengths, rope_dim)
        caches = [cache0, cache1]
        new_caches = []
        x_rows = x
        for layer_idx in range(len(caches)):
            attn_part, new_cache = attention_local(x_rows, lengths, caches[layer_idx], cos_tab, sin_tab, attn_gain[layer_idx], kv_gain[layer_idx], q_gain[layer_idx], w_dkv[layer_idx], w_qa[layer_idx], w_qb[layer_idx], w_uk[layer_idx], w_uv[layer_idx], w_o[layer_idx])
            attn_out = lax.psum(attn_part, 'tp')
            x_mid = (x_rows.astype(jnp.float32) + attn_out).astype(jnp.bfloat16)
            ffn_in = rms_norm(x_mid, ffn_gain[layer_idx])
            all_in = lax.all_gather(ffn_in, 'dp', axis=0, tiled=True)
            gate_cols = lax.dynamic_slice(w_gate, (layer_idx, 0, ffn_start), (1, model_dim, ffn_width))[0]
            up_cols = lax.dynamic_slice(w_up, (layer_idx, 0, ffn_start), (1, model_dim, ffn_width))[0]
            down_rows = lax.dynamic_slice(w_down, (layer_idx, ffn_start, 0), (1, ffn_width, model_dim))[0]
            hidden = (jax.nn.silu(jnp.dot(all_in, gate_cols, preferred_element_type=jnp.float32)) * jnp.dot(all_in, up_cols, preferred_element_type=jnp.float32)).astype(jnp.bfloat16)
            ffn_partial = jnp.dot(hidden, down_rows, preferred_element_type=jnp.float32).astype(jnp.bfloat16)
            received = lax.all_to_all(ffn_partial, 'dp', 0, 0, tiled=True)
            rank_sum = jnp.sum(received.reshape(dp_size, row_count, model_dim).astype(jnp.float32), axis=0)
            ffn_out = lax.psum(rank_sum, 'tp')
            x_rows = (x_mid.astype(jnp.float32) + ffn_out).astype(jnp.bfloat16)
            new_caches.append(new_cache)
        return x_rows, new_caches[0], new_caches[1]

    return jax.shard_map(local_step, mesh=mesh, in_specs=in_specs, out_specs=out_specs, check_vma=False)
```

profile of v0, /device:TPU:0, one launch (start us, length us, event | category | flops | bytes accessed | tf_op | source)
XLA Modules:
  0.0 298.7 jit_solution(14801391905672881262)
XLA Ops:
  7.8 1.5 convert_element_type.123
  12.4 1.4 fusion.169
  13.8 1.4 slice_reduce_fusion
  15.2 2.5 fusion.34
  19.1 4.9 %multiply_reduce_fusion.1 = (f32[32]{0:T(128)S(1)}, f32[32,1536]{1,0:T(8,128)}) fusion(bf16[2,2048,1536]{2,1,0:T(8,128)(2,1)} %param.26, bf16[32,2048]{1,0:T(8,128)(2,1)} %param.17, f32[2048]{0:T(1024)S(1)} %bitcast.137, f32[32]{0:T(128)S(1)} %add_rsqrt_fusion.7), kind=kOutput, calls=%fused_computation.115 | convolution fusion | flops 201687008 | bytes 6627584 | tf_op jit(solution)/shard_map/dot_general | solution.py:40
  24.5 2.5 slice_bitcast_fusion
  27.0 2.8 copy.26
  29.8 1.8 fusion.115
  34.1 6.4 %broadcast_select_fusion.1 = bf16[32,256,576]{1,2,0:T(8,128)(2,1)S(1)} fusion(bf16[32,256,576]{1,2,0:T(8,128)(2,1)} %param.19, pred[32,256]{1,0:T(8,128)(4,1)S(1)} %get-tuple-element.32, bf16[32,576]{1,0:T(8,128)(2,1)S(1)} %pad_maximum_fusion), kind=kLoop, calls=%fused_computation.3 | loop fusion | flops 4718592 | bytes 18919424 | tf_op jit(solution)/shard_map/jit(_where)/select_n | solution.py:39
  41.8 2.4 copy-done
  44.5 6.3 %fusion.124 = bf16[32,4,576]{2,1,0:T(4,128)(2,1)S(1)} fusion(bf16[32,256,576]{1,2,0:T(8,128)(2,1)} %copy-done, f32[32,4]{1,0:T(8,128)S(1)} %fusion.171, f32[32,4,256]{2,1,0:T(4,128)S(1)} %fusion.61), kind=kOutput, calls=%fused_computation.140 | convolution fusion | flops 37847424 | bytes 9716224 | tf_op jit(solution)/shard_map/bht,btk->bhk/dot_general | solution.py:49
  51.1 2.8 fusion.40
  54.6 37.7 %all-reduce.5.cloned.1.call-done = f32[32,2048]{1,0:T(8,128)} async-done(((f32[32,2048]{1,0:T(8,128)}), f32[32,2048]{1,0:T(8,128)}) %all-reduce.5.cloned.1.call-update) | async-done | bytes 262160 | tf_op jit(solution)/shard_map/psum | solution.py:74
  93.4 7.4 %all_gather.6 = bf16[128,2048]{1,0:T(8,128)(2,1)S(1)} all-gather(bf16[32,2048]{1,0:T(8,128)(2,1)S(1)} %fusion.92), channel_id=1, replica_groups=mesh['rep'=2,'tp'=4,'dp'=4] {'dp'}, dimensions={0}, use_global_device_ids=true | all-gather | bytes 655360 | tf_op jit(solution)/shard_map/all_gather | solution.py:77
  100.8 4.7 %fusion.14 = f32[128,704]{0,1:T(8,128)S(1)} fusion(bf16[128,2048]{1,0:T(8,128)(2,1)S(1)} %all_gather.6, bf16[2,2048,11264]{2,1,0:T(8,128)(2,1)} %param.31, s32[]{:T(128)S(6)} %select_n.24), kind=kOutput, calls=%fused_computation.16 | convolution fusion | flops 369098752 | bytes 4030468 | tf_op jit(solution)/shard_map/dot_general | solution.py:81
  105.5 6.6 %fusion.26 = bf16[128,2048]{1,0:T(8,128)(2,1)S(1)} fusion(bf16[2,11264,2048]{2,1,0:T(8,128)(2,1)} %param.33, s32[]{:T(128)S(6)} %select_n.24, bf16[128,2048]{1,0:T(8,128)(2,1)S(1)} %all_gather.6, bf16[2,2048,11264]{2,1,0:T(8,128)(2,1)} %param.32, f32[128,704]{0,1:T(8,128)S(1)} %fusion.14), kind=kOutput, calls=%fused_computation.28 | convolution fusion | flops 739000320 | bytes 7439360 | tf_op jit(solution)/shard_map/dot_general | solution.py:82
  112.2 11.2 %all_to_all.18 = bf16[4,32,2048]{2,1,0:T(8,128)(2,1)S(1)} all-to-all(bf16[4,32,2048]{2,1,0:T(8,128)(2,1)S(1)} %bitcast.127), channel_id=1, replica_groups=mesh['rep'=2,'tp'=4,'dp'=4] {'dp'}, dimensions={0} | all-to-all | bytes 1048576 | tf_op jit(solution)/shard_map/all_to_all | solution.py:83
  124.5 2.8 copy.30
  127.3 31.3 %all-reduce.7.cloned.1.call-done = f32[32,2048]{1,0:T(8,128)} async-done(((f32[32,2048]{1,0:T(8,128)}), f32[32,2048]{1,0:T(8,128)}) %all-reduce.7.cloned.1.call-update) | async-done | bytes 262160 | tf_op jit(solution)/shard_map/psum | solution.py:85
  159.8 2.5 fusion.32
  163.2 4.1 %multiply_reduce_fusion = (f32[32]{0:T(128)S(1)}, f32[32,1536]{1,0:T(8,128)S(1)}) fusion(bf16[2,2048,1536]{2,1,0:T(8,128)(2,1)} %param.26, bf16[32,2048]{1,0:T(8,128)(2,1)S(1)} %get-tuple-element.8, f32[2048]{0:T(1024)} %bitcast.135, f32[32]{0:T(128)S(1)} %add_rsqrt_fusion.3), kind=kOutput, calls=%fused_computation.113 | convolution fusion | flops 201687008 | bytes 6627584 | tf_op jit(solution)/shard_map/dot_general | solution.py:40
  168.9 6.4 %broadcast_select_fusion = bf16[32,256,576]{1,2,0:T(8,128)(2,1)S(1)} fusion(bf16[32,256,576]{1,2,0:T(8,128)(2,1)} %param.20, pred[32,256]{1,0:T(8,128)(4,1)S(1)} %get-tuple-element.32, bf16[32,576]{1,0:T(8,128)(2,1)S(1)} %pad_maximum_fusion.1), kind=kLoop, calls=%fused_computation.2 | loop fusion | flops 4718592 | bytes 18919424 | tf_op jit(solution)/shard_map/jit(_where)/select_n | solution.py:39
  176.7 2.4 copy-done.1
  179.3 6.3 %fusion.125 = bf16[32,4,576]{2,1,0:T(4,128)(2,1)S(1)} fusion(bf16[32,256,576]{1,2,0:T(8,128)(2,1)} %copy-done.1, f32[32,4]{1,0:T(8,128)S(1)} %fusion.172, f32[32,4,256]{2,1,0:T(4,128)S(1)} %fusion.60), kind=kOutput, calls=%fused_computation.141 | convolution fusion | flops 37847424 | bytes 9716224 | tf_op jit(solution)/shard_map/bht,btk->bhk/dot_general | solution.py:49
  186.0 2.8 fusion.38
  188.8 35.3 %all-reduce.9.cloned.1.call-done = f32[32,2048]{1,0:T(8,128)} async-done(((f32[32,2048]{1,0:T(8,128)}), f32[32,2048]{1,0:T(8,128)}) %all-reduce.9.cloned.1.call-update) | async-done | bytes 262160 | tf_op jit(solution)/shard_map/psum | solution.py:74
  225.3 7.4 %all_gather.7 = bf16[128,2048]{1,0:T(8,128)(2,1)S(1)} all-gather(bf16[32,2048]{1,0:T(8,128)(2,1)S(1)} %fusion.100), channel_id=1, replica_groups=mesh['rep'=2,'tp'=4,'dp'=4] {'dp'}, dimensions={0}, use_global_device_ids=true | all-gather | bytes 655360 | tf_op jit(solution)/shard_map/all_gather | solution.py:77
  232.8 4.7 %fusion.10 = f32[128,704]{0,1:T(8,128)S(1)} fusion(bf16[128,2048]{1,0:T(8,128)(2,1)S(1)} %all_gather.7, bf16[2,2048,11264]{2,1,0:T(8,128)(2,1)} %param.31, s32[]{:T(128)S(6)} %select_n.24), kind=kOutput, calls=%fused_computation.12 | convolution fusion | flops 369098752 | bytes 4030468 | tf_op jit(solution)/shard_map/dot_general | solution.py:81
  237.5 6.6 %fusion.29 = bf16[128,2048]{1,0:T(8,128)(2,1)S(1)} fusion(bf16[2,11264,2048]{2,1,0:T(8,128)(2,1)} %param.33, s32[]{:T(128)S(6)} %select_n.24, bf16[128,2048]{1,0:T(8,128)(2,1)S(1)} %all_gather.7, bf16[2,2048,11264]{2,1,0:T(8,128)(2,1)} %param.32, f32[128,704]{0,1:T(8,128)S(1)} %fusion.10), kind=kOutput, calls=%fused_computation.29 | convolution fusion | flops 739000320 | bytes 7439360 | tf_op jit(solution)/shard_map/dot_general | solution.py:82
  244.1 11.2 %all_to_all.19 = bf16[4,32,2048]{2,1,0:T(8,128)(2,1)S(1)} all-to-all(bf16[4,32,2048]{2,1,0:T(8,128)(2,1)S(1)} %bitcast.126), channel_id=1, replica_groups=mesh['rep'=2,'tp'=4,'dp'=4] {'dp'}, dimensions={0} | all-to-all | bytes 1048576 | tf_op jit(solution)/shard_map/all_to_all | solution.py:83
  256.1 34.4 %all-reduce.11.cloned.1.call-done = f32[32,2048]{1,0:T(8,128)} async-done(((f32[32,2048]{1,0:T(8,128)}), f32[32,2048]{1,0:T(8,128)}) %all-reduce.11.cloned.1.call-update) | async-done | bytes 262160 | tf_op jit(solution)/shard_map/psum | solution.py:85
  290.5 1.6 fusion.101
  (89 shorter events, 20.1 us)
Async XLA Ops:
  7.2 85.1 %all-reduce.5.cloned.1.call-start = ((), (), s32[]{:S(2)}) async-start(), calls=%async_computation.2 | async-start | bytes 524288 | tf_op jit(solution)/shard_map/psum | solution.py:74
  7.2 17.3 %copy-start.2 = (bf16[2,1536,768]{2,1,0:T(8,128)(2,1)S(1)}, bf16[2,1536,768]{2,1,0:T(8,128)(2,1)}, u32[]{:S(2)}) copy-start(bf16[2,1536,768]{2,1,0:T(8,128)(2,1)} %param.27) | copy-start | bytes 14155780
  17.8 0.7 copy-start.7
  24.5 7.1 %copy-start.3 = (bf16[2,4,128,512]{3,2,1,0:T(8,128)(2,1)S(1)}, bf16[2,4,128,512]{3,2,1,0:T(8,128)(2,1)}, u32[]{:S(2)}) copy-start(bf16[2,4,128,512]{3,2,1,0:T(8,128)(2,1)} %param.28) | copy-start | bytes 3145732
  32.9 1.1 copy-start.8
  32.9 1.1 copy-start.10
  40.5 3.7 %copy-start = (bf16[32,256,576]{1,2,0:T(8,128)(2,1)}, bf16[32,256,576]{1,2,0:T(8,128)(2,1)S(1)}, u32[]{:S(2)}) copy-start(bf16[32,256,576]{1,2,0:T(8,128)(2,1)S(1)} %broadcast_select_fusion.1) | copy-start | bytes 28311556
  44.2 6.7 %copy-start.16 = (bf16[2,4,512,128]{3,2,1,0:T(8,128)(2,1)S(1)}, bf16[2,4,512,128]{3,2,1,0:T(8,128)(2,1)}, u32[]{:S(2)}) copy-start(bf16[2,4,512,128]{3,2,1,0:T(8,128)(2,1)} %param.29) | copy-start | bytes 3145732
  44.4 9.5 %copy-start.14 = (f32[2,2048]{1,0:T(2,128)S(1)}, f32[2,2048]{1,0:T(2,128)}, u32[]{:S(2)}) copy-start(f32[2,2048]{1,0:T(2,128)} %param.24) | copy-start | bytes 49156
  44.4 47.8 %copy-start.6 = (bf16[32,2048]{1,0:T(8,128)(2,1)S(1)}, bf16[32,2048]{1,0:T(8,128)(2,1)}, u32[]{:S(2)}) copy-start(bf16[32,2048]{1,0:T(8,128)(2,1)} %param.17) | copy-start | bytes 393220
  53.9 104.7 %all-reduce.7.cloned.1.call-start = ((), (), s32[]{:S(2)}) async-start(), calls=%async_computation.3 | async-start | bytes 524288 | tf_op jit(solution)/shard_map/psum | solution.py:85
  124.2 99.9 %all-reduce.9.cloned.1.call-start = ((), (), s32[]{:S(2)}) async-start(), calls=%async_computation.4 | async-start | bytes 524288 | tf_op jit(solution)/shard_map/psum | solution.py:74
  158.6 8.8 %copy-start.12 = (f32[1536]{0:T(1024)S(1)}, f32[1536]{0:T(1024)}, u32[]{:S(2)}) copy-start(f32[1536]{0:T(1024)} %get-tuple-element.3) | copy-start | bytes 18436
  159.7 8.6 %copy-start.4 = (bf16[32,2048]{1,0:T(8,128)(2,1)}, bf16[32,2048]{1,0:T(8,128)(2,1)S(1)}, u32[]{:S(2)}) copy-start(bf16[32,2048]{1,0:T(8,128)(2,1)S(1)} %get-tuple-element.8) | copy-start | bytes 393220
  159.7 8.5 %copy-start.9 = (f32[32,32]{1,0:T(8,128)S(1)}, f32[32,32]{1,0:T(8,128)}, u32[]{:S(2)}) copy-start(f32[32,32]{1,0:T(8,128)} %copy-done.8) | copy-start | bytes 12292
  159.7 8.5 %copy-start.11 = (f32[32,32]{1,0:T(8,128)S(1)}, f32[32,32]{1,0:T(8,128)}, u32[]{:S(2)}) copy-start(f32[32,32]{1,0:T(8,128)} %copy-done.10) | copy-start | bytes 12292
  159.8 9.0 %copy-start.15 = (f32[1,512]{1,0:T(1,128)S(1)}, f32[1,512]{1,0:T(1,128)}, u32[]{:S(2)}) copy-start(f32[1,512]{1,0:T(1,128)} %get-tuple-element.25) | copy-start | bytes 6148
  175.3 3.7 %copy-start.1 = (bf16[32,256,576]{1,2,0:T(8,128)(2,1)}, bf16[32,256,576]{1,2,0:T(8,128)(2,1)S(1)}, u32[]{:S(2)}) copy-start(bf16[32,256,576]{1,2,0:T(8,128)(2,1)S(1)} %broadcast_select_fusion) | copy-start | bytes 28311556
  179.1 6.7 %copy-start.17 = (bf16[2,4,512,128]{3,2,1,0:T(8,128)(2,1)S(1)}, bf16[2,4,512,128]{3,2,1,0:T(8,128)(2,1)}, u32[]{:S(2)}) copy-start(bf16[2,4,512,128]{3,2,1,0:T(8,128)(2,1)} %param.29) | copy-start | bytes 3145732
  179.3 44.8 %copy-start.5 = (bf16[32,2048]{1,0:T(8,128)(2,1)S(1)}, bf16[32,2048]{1,0:T(8,128)(2,1)}, u32[]{:S(2)}) copy-start(bf16[32,2048]{1,0:T(8,128)(2,1)} %copy-done.4) | copy-start | bytes 393220
  179.3 45.9 %copy-start.13 = (f32[1,2048]{1,0:T(1,128)S(1)}, f32[1,2048]{1,0:T(1,128)}, u32[]{:S(2)}) copy-start(f32[1,2048]{1,0:T(1,128)} %get-tuple-element.21) | copy-start | bytes 24580
  188.7 101.8 %all-reduce.11.cloned.1.call-start = ((), (), s32[]{:S(2)}) async-start(), calls=%async_computation.5 | async-start | bytes 524288 | tf_op jit(solution)/shard_map/psum | solution.py:85
Sparse Core Ops, SparseCore 0:
  54.0 38.1 all-reduce.4
  124.3 34.2 all-reduce.6
  188.9 35.1 all-reduce.8
  256.2 34.2 all-reduce.10
where the time goes:
time: 300 us; the launch traced here: 299 us
  waiting for transfers between devices  139 us (46%)
  matrix products  61 us (20%)
  blocking collectives  37.2 us (12%)
  other arithmetic  28.2 us (9%)
  local copies, waits for them, and re-layouts  18.9 us (6%)
  between operations  14.2 us (5%)
    psum x2, waiting for transfers between devices, local_step(): attn_out = lax.psum(attn_part, 'tp')  73 us
    psum x2, waiting for transfers between devices, local_step(): ffn_out = lax.psum(rank_sum, 'tp')  65.7 us
    all_to_all x2, blocking collectives, local_step(): received = lax.all_to_all(ffn_partial, 'dp', 0, 0, tiled=True)  22.4 us
    all_gather x2, blocking collectives, local_step(): all_in = lax.all_gather(ffn_in, 'dp', axis=0, tiled=True)  14.8 us
    dot_general x2, matrix products, local_step(): jnp.dot(hidden, down_rows, preferred_element_type=jnp.float32)  13.2 us
    select_n x2, other arithmetic, attention_local(): new_cache = jnp.where(is_slot, new_entry[:, None, :], cache)  12.8 us
    dot_general x2, matrix products, attention_local(): jnp.einsum('bht,btk->bhk', att_probs, new_cache, preferred_element_type=j...  12.7 us
    dot_general x2, matrix products, local_step(): jnp.dot(all_in, gate_cols, preferred_element_type=jnp.float32)  9.46 us
  transfers between devices with their start and end apart: 4, of which 4 were waited for; matrix products, arithmetic and copies ran while one was open for 1% of the time, Pallas kernels for 0%

commit v1 on v0

v1 whole, which is shorter than its diff:
```python
import functools

import jax
import jax.numpy as jnp
from jax import lax
from jax.experimental import pallas as pl
from jax.experimental.pallas import tpu as pltpu
from jax.sharding import PartitionSpec as P

MESH = pl.DeviceIdType.MESH
EPS = 1e-6
LOG_BASE = 9.210340371976184
F32 = jnp.float32
BF16 = jnp.bfloat16
NT = (((1,), (1,)), ((), ()))
VMEM_LIMIT = 60 * 1024 * 1024


def mm(a, b):
    return jnp.dot(a, b, preferred_element_type=F32)


def rms(v, gain):
    inv = lax.rsqrt(jnp.mean(v * v, axis=-1, keepdims=True) + EPS)
    return (v * inv * gain).astype(BF16)


def attn_kernel(layer, x_ref, len_s, len_v, ag_ref, kg_ref, qg_ref, cache, w_dkv, w_qa, w_qb, w_uk, w_uv, w_o, part_ref, out_cache,
                c_v, dkv_v, qa_v, qb_v, uk_v, uv_v, o_v, qlow_s, ent_s, qs, qb16, sc_s, p_s, os, ho_s, wsem, csem, osem):
    rows, lat, rope, heads, qk = 32, 512, 64, 4, 192
    slots = c_v.shape[2]
    per = 4
    groups = rows // per
    width = 512
    qa_n = qa_v.shape[1] // width
    copies = []
    for n in range(qa_n):
        copies.append(pltpu.make_async_copy(w_qa.at[layer, :, pl.ds(n * width, width)], qa_v.at[:, pl.ds(n * width, width)], wsem.at[n]))
    copies.append(pltpu.make_async_copy(w_dkv.at[layer], dkv_v, wsem.at[qa_n]))
    copies.append(pltpu.make_async_copy(w_qb.at[layer], qb_v, wsem.at[qa_n + 1]))
    copies.append(pltpu.make_async_copy(w_uk.at[layer], uk_v, wsem.at[qa_n + 2]))
    copies.append(pltpu.make_async_copy(w_uv.at[layer], uv_v, wsem.at[qa_n + 3]))
    copies.append(pltpu.make_async_copy(w_o.at[layer], o_v, wsem.at[qa_n + 4]))

    def cache_in(g):
        return pltpu.make_async_copy(cache.at[pl.ds(g * per, per)], c_v.at[pl.ds(g * per, per)], csem.at[g])

    def cache_out(g):
        return pltpu.make_async_copy(c_v.at[pl.ds(g * per, per)], out_cache.at[pl.ds(g * per, per)], osem.at[g])

    for n in range(qa_n + 3):
        copies[n].start()

    xf = x_ref[...].astype(F32)
    h = rms(xf, ag_ref[layer:layer + 1, :])

    half = rope // 2
    lens_row = len_v[...].astype(F32)
    freq_t = jnp.exp(lax.broadcasted_iota(jnp.int32, (half, rows), 0).astype(F32) * (-LOG_BASE / half))
    ang_t = freq_t * jnp.broadcast_to(lens_row, (half, rows))
    cos_t, sin_t = jnp.cos(ang_t), jnp.sin(ang_t)
    cos_r, sin_r = cos_t.T, sin_t.T

    ssq = jnp.zeros((rows, 1), F32)
    for n in range(qa_n):
        copies[n].wait()
        if n == 0:
            for g in range(2):
                cache_in(g).start()
        part = mm(h, qa_v[:, n * width:(n + 1) * width])
        ssq = ssq + jnp.sum(part * part, axis=-1, keepdims=True)
        qlow_s[:, n * width:(n + 1) * width] = part
    for g in range(2, groups):
        cache_in(g).start()
    copies[qa_n].wait()
    kt = lax.dot_general(dkv_v[...], h, NT, preferred_element_type=F32)
    kl = kt[:lat]
    inv_k = lax.rsqrt(jnp.mean(kl * kl, axis=0, keepdims=True) + EPS)
    gain_t = jnp.broadcast_to(kg_ref[layer:layer + 1, :], (128, lat)).T[:, :rows]
    ent_s[0:lat, 0:rows] = (kl * inv_k * gain_t).astype(BF16).astype(F32)
    ka, kb = kt[lat:lat + half], kt[lat + half:]
    ent_s[lat:lat + half, 0:rows] = (ka * cos_t - kb * sin_t).astype(BF16).astype(F32)
    ent_s[lat + half:, 0:rows] = (kb * cos_t + ka * sin_t).astype(BF16).astype(F32)

    inv_q = lax.rsqrt(ssq / (qa_n * width) + EPS)
    copies[qa_n + 1].wait()
    q_low = (qlow_s[...] * inv_q * qg_ref[layer:layer + 1, :]).astype(BF16)
    q_full = mm(q_low, qb_v[...])
    copies[qa_n + 2].wait()
    for hd in range(heads):
        qh = q_full[:, hd * qk:(hd + 1) * qk]
        q_lat = mm(qh[:, :128].astype(BF16), uk_v[hd])
        for c in range(lat // 128):
            qs[c, pl.ds(hd, rows, stride=heads), :] = q_lat[:, c * 128:(c + 1) * 128]
        qa, qb = qh[:, 128:128 + half], qh[:, 128 + half:]
        rot = jnp.concatenate([qa * cos_r - qb * sin_r, qb * cos_r + qa * sin_r, jnp.zeros((rows, 128 - rope), F32)], axis=-1)
        qs[lat // 128, pl.ds(hd, rows, stride=heads), :] = rot
    for c in range(lat // 128 + 1):
        qb16[:, c * 128:(c + 1) * 128] = qs[c].astype(BF16)
    copies[qa_n + 3].start()
    copies[qa_n + 4].start()

    lane = lax.broadcasted_iota(jnp.int32, (1, slots), 1)
    lane_full = lax.broadcasted_iota(jnp.int32, (per * heads, slots), 1)
    row_of = lax.broadcasted_iota(jnp.int32, (per * heads, 1), 0) // heads
    row_w = lax.broadcasted_iota(jnp.int32, (per * heads, slots), 0) // heads
    row_l = lax.broadcasted_iota(jnp.int32, (per * heads, lat), 0) // heads
    scale = float(qk) ** -0.5

    def score_group(g):
        q16 = qb16[pl.ds(pl.multiple_of(g * 16, 16), 16), 0:lat + rope]
        ent = ent_s[...]
        acc = None
        for i in range(per):
            r = g * per + i
            n_r = len_s[r]
            col = jnp.broadcast_to(ent[:, i:i + 1], (lat + rope, slots)).astype(BF16)
            hit = jnp.broadcast_to(lane == n_r, (lat + rope, slots))
            new = jnp.where(hit, col, c_v[r])
            c_v[r] = new
            s_i = mm(q16, new) * scale
            s_i = jnp.where(lane_full <= n_r, s_i, -1e30)
            acc = s_i if acc is None else jnp.where(row_w == i, s_i, acc)
        ent_s[...] = pltpu.roll(ent, 128 - per, 1)
        sc_s[pl.ds(pl.multiple_of(g * 16, 16), 16), :] = acc

    def score_loop(g, c):
        cache_in(g).wait()
        score_group(g)
        cache_out(g).start()
        return c

    lax.fori_loop(0, groups, score_loop, 0)
    s = sc_s[...]
    e = jnp.exp(s - jnp.max(s, axis=-1, keepdims=True))
    p_s[...] = (e / jnp.sum(e, axis=-1, keepdims=True)).astype(BF16)

    def out_loop(g, c):
        p16 = p_s[pl.ds(pl.multiple_of(g * 16, 16), 16), :]
        acc = None
        for i in range(per):
            o_i = lax.dot_general(p16, c_v[g * per + i, 0:lat, :], NT, preferred_element_type=F32)
            acc = o_i if acc is None else jnp.where(row_l == i, o_i, acc)
        for c in range(lat // 128):
            os[c, pl.ds(pl.multiple_of(g * 16, 16), 16), :] = acc[:, c * 128:(c + 1) * 128]
        return c

    lax.fori_loop(0, groups, out_loop, 0)
    copies[qa_n + 3].wait()
    for hd in range(heads):
        o_lat = jnp.concatenate([os[c, pl.ds(hd, rows, stride=heads), :].astype(BF16) for c in range(lat // 128)], axis=-1)
        ho_s[:, hd * 128:(hd + 1) * 128] = mm(o_lat, uv_v[hd]).astype(BF16)
    copies[qa_n + 4].wait()
    ho = ho_s[...]
    for n in range(4):
        part_ref[:, n * 512:(n + 1) * 512] = mm(ho, o_v[:, n * 512:(n + 1) * 512])
    for g in range(groups):
        cache_out(g).wait()


def attn_call(layer, x, lengths, attn_gain, kv_gain, q_gain, cache_t, w_dkv_t, w_qa, w_qb, w_uk, w_uv, w_o):
    any_spec = pl.BlockSpec(memory_space=pl.ANY)
    vmem = pl.BlockSpec(memory_space=pltpu.VMEM)
    smem = pl.BlockSpec(memory_space=pltpu.SMEM)
    rows, width, slots = cache_t.shape
    heads = w_uk.shape[1]
    return pl.pallas_call(
        functools.partial(attn_kernel, layer),
        out_shape=(jax.ShapeDtypeStruct(x.shape, F32), jax.ShapeDtypeStruct(cache_t.shape, BF16)),
        in_specs=[vmem, smem, vmem, vmem, vmem, vmem] + [any_spec] * 7,
        out_specs=(vmem, any_spec),
        scratch_shapes=[
            pltpu.VMEM(cache_t.shape, BF16),
            pltpu.VMEM(w_dkv_t.shape[1:], BF16),
            pltpu.VMEM(w_qa.shape[1:], BF16),
            pltpu.VMEM(w_qb.shape[1:], BF16),
            pltpu.VMEM(w_uk.shape[1:], BF16),
            pltpu.VMEM(w_uv.shape[1:], BF16),
            pltpu.VMEM(w_o.shape[1:], BF16),
            pltpu.VMEM((rows, w_qa.shape[2]), F32),
            pltpu.VMEM((width, 128), F32),
            pltpu.VMEM((5, rows * heads, 128), F32),
            pltpu.VMEM((rows * heads, 640), BF16),
            pltpu.VMEM((rows * heads, slots), F32),
            pltpu.VMEM((rows * heads, slots), BF16),
            pltpu.VMEM((4, rows * heads, 128), F32),
            pltpu.VMEM((rows, heads * 128), BF16),
            pltpu.SemaphoreType.DMA((8,)),
            pltpu.SemaphoreType.DMA((8,)),
            pltpu.SemaphoreType.DMA((8,)),
        ],
        compiler_params=pltpu.CompilerParams(vmem_limit_bytes=VMEM_LIMIT),
        cost_estimate=pl.CostEstimate(flops=2_000_000_000, bytes_accessed=33_000_000, transcendentals=0),
        name=f"attn{layer}",
    )(x, lengths, lengths.reshape(1, rows), attn_gain, kv_gain, q_gain, cache_t, w_dkv_t, w_qa, w_qb, w_uk, w_uv, w_o)


def ffn_kernel(layer, n_tp, n_dp, part_ref, x_ref, fg_ref, w_gate, w_up, w_down, out_ref,
               g_v, u_v, d_v, rs_buf, xm_s, g_snd, g_buf, hid, f_snd, f_buf, x_snd,
               wsem, s_rs, r_rs, s_g, r_g, s_f, r_f, s_x, r_x):
    z = lax.axis_index("tp")
    d = lax.axis_index("dp")
    hid_w = g_v.shape[1]
    start = pl.multiple_of(d * hid_w, hid_w)
    half = hid_w // 2
    loads = []
    for c in range(2):
        loads.append(pltpu.make_async_copy(w_gate.at[layer, :, pl.ds(pl.multiple_of(start + c * half, 128), half)], g_v.at[:, pl.ds(c * half, half)], wsem.at[3 * c]))
        loads.append(pltpu.make_async_copy(w_up.at[layer, :, pl.ds(pl.multiple_of(start + c * half, 128), half)], u_v.at[:, pl.ds(c * half, half)], wsem.at[3 * c + 1]))
    for c in range(2):
        loads.append(pltpu.make_async_copy(w_down.at[layer, pl.ds(start + c * half, half), :], d_v.at[pl.ds(c * half, half), :], wsem.at[3 * c + 2]))
    for cp in loads:
        cp.start()

    tp_peers = [lax.rem(z + k, n_tp) for k in range(1, n_tp)]
    dp_peers = [lax.rem(d + k, n_dp) for k in range(1, n_dp)]
    barrier = pltpu.get_barrier_semaphore()
    for pz in tp_peers:
        pl.semaphore_signal(barrier, inc=1, device_id={"tp": pz}, device_id_type=MESH)
    for pd in dp_peers:
        pl.semaphore_signal(barrier, inc=1, device_id={"dp": pd}, device_id_type=MESH)
    pl.semaphore_wait(barrier, n_tp + n_dp - 2)

    def exchange(peers, axis, src_of, dst_of, ssem, rsem):
        cps = []
        for k, p in enumerate(peers):
            cps.append(pltpu.make_async_remote_copy(src_ref=src_of(k, p), dst_ref=dst_of(k), send_sem=ssem.at[k], recv_sem=rsem.at[k], device_id={axis: p}, device_id_type=MESH))
        return cps

    rs = exchange(tp_peers, "tp", lambda k, p: part_ref.at[p], lambda k: rs_buf.at[k], s_rs, r_rs)
    for cp in rs:
        cp.start()
    acc = x_ref[z].astype(F32)
    tot = part_ref[z]
    for k, cp in enumerate(rs):
        cp.wait_recv()
        tot = tot + rs_buf[k]
    xm = (acc + tot).astype(BF16).astype(F32)
    xm_s[...] = xm
    g = rms(xm, fg_ref[layer:layer + 1, :])
    g_snd[...] = g
    gx = exchange(dp_peers, "dp", lambda k, p: g_snd, lambda k: g_buf.at[k], s_g, r_g)
    for cp in gx:
        cp.start()
    for cp in gx:
        cp.wait_recv()
    full = jnp.concatenate([g.astype(F32)] + [g_buf[k].astype(F32) for k in range(n_dp - 1)], axis=0).astype(BF16)

    tile = 256
    for j in range(hid_w // tile):
        if j == 0:
            loads[0].wait()
            loads[1].wait()
        if (j + 1) * tile > half and j * tile <= half:
            loads[2].wait()
            loads[3].wait()
        gate = mm(full, g_v[:, j * tile:(j + 1) * tile])
        up = mm(full, u_v[:, j * tile:(j + 1) * tile])
        hid[:, j * tile:(j + 1) * tile] = (gate * jax.nn.sigmoid(gate) * up).astype(BF16)
    loads[4].wait()
    loads[5].wait()
    hv = hid[...]
    own = []
    for j in range(4):
        y = mm(hv, d_v[:, j * 512:(j + 1) * 512])
        for k in range(n_dp):
            f_snd[k, :, j * 512:(j + 1) * 512] = y[k * 8:(k + 1) * 8].astype(BF16)
    fx = []
    for k, p in enumerate(dp_peers):
        fx.append(pltpu.make_async_remote_copy(src_ref=f_snd.at[n_dp - 1 - k], dst_ref=f_buf.at[k], send_sem=s_f.at[k], recv_sem=r_f.at[k], device_id={"dp": p}, device_id_type=MESH))
    for cp in fx:
        cp.start()
    tot = f_snd[0].astype(F32)
    for k, cp in enumerate(fx):
        cp.wait_recv()
        tot = tot + f_buf[k].astype(F32)
    x_new = (xm_s[...] + tot).astype(BF16)
    x_snd[...] = x_new
    out_ref[z] = x_new
    xx = exchange(tp_peers, "tp", lambda k, p: x_snd, lambda k: out_ref.at[z], s_x, r_x)
    for cp in xx:
        cp.start()
    for cp in xx:
        cp.wait_recv()
    for cp in rs + gx + fx + xx:
        cp.wait_send()


def ffn_call(layer, n_tp, n_dp, part, x, ffn_gain, w_gate, w_up, w_down):
    any_spec = pl.BlockSpec(memory_space=pl.ANY)
    vmem = pl.BlockSpec(memory_space=pltpu.VMEM)
    rows, dim = x.shape
    own = rows // n_tp
    hid_w = w_gate.shape[2] // n_dp
    dma = pltpu.SemaphoreType.DMA
    out = pl.pallas_call(
        functools.partial(ffn_kernel, layer, n_tp, n_dp),
        out_shape=jax.ShapeDtypeStruct((n_tp, own, dim), BF16),
        in_specs=[vmem, vmem, vmem] + [any_spec] * 3,
        out_specs=vmem,
        scratch_shapes=[
            pltpu.VMEM((dim, hid_w), BF16),
            pltpu.VMEM((dim, hid_w), BF16),
            pltpu.VMEM((hid_w, dim), BF16),
            pltpu.VMEM((n_tp - 1, own, dim), F32),
            pltpu.VMEM((own, dim), F32),
            pltpu.VMEM((own, dim), BF16),
            pltpu.VMEM((n_dp - 1, own, dim), BF16),
            pltpu.VMEM((own * n_dp, hid_w), BF16),
            pltpu.VMEM((n_dp, own, dim), BF16),
            pltpu.VMEM((n_dp - 1, own, dim), BF16),
            pltpu.VMEM((own, dim), BF16),
            dma((6,)), dma((3,)), dma((3,)), dma((3,)), dma((3,)), dma((3,)), dma((3,)), dma((3,)), dma((3,)),
        ],
        compiler_params=pltpu.CompilerParams(vmem_limit_bytes=VMEM_LIMIT, collective_id=layer, has_side_effects=True),
        cost_estimate=pl.CostEstimate(flops=1_100_000_000, bytes_accessed=35_000_000, transcendentals=0),
        name=f"ffn{layer}",
    )(part.reshape(n_tp, own, dim), x.reshape(n_tp, own, dim), ffn_gain, w_gate, w_up, w_down)
    return out.reshape(rows, dim)


def solution(mesh):
    n_tp = mesh.shape["tp"]
    n_dp = mesh.shape["dp"]
    row_spec = P(("rep", "dp"), None)
    cache_spec = P(("rep", "dp"), None, None)
    in_specs = (row_spec, P(("rep", "dp")), cache_spec, cache_spec, P(), P(), P(), P(), P(), P(), P(None, None, "tp"), P(None, "tp", None, None), P(None, "tp", None, None), P(None, "tp", None), P(), P(), P())
    out_specs = (row_spec, cache_spec, cache_spec)

    def local_step(x, lengths, cache0, cache1, attn_gain, kv_gain, q_gain, ffn_gain, w_dkv, w_qa, w_qb, w_uk, w_uv, w_o, w_gate, w_up, w_down):
        w_dkv_t = jnp.swapaxes(w_dkv, 1, 2)
        new_caches = []
        for layer, cache in enumerate((cache0, cache1)):
            part, new_cache = attn_call(layer, x, lengths, attn_gain, kv_gain, q_gain, jnp.swapaxes(cache, 1, 2), w_dkv_t, w_qa, w_qb, w_uk, w_uv, w_o)
            x = ffn_call(layer, n_tp, n_dp, part, x, ffn_gain, w_gate, w_up, w_down)
            new_caches.append(jnp.swapaxes(new_cache, 1, 2))
        return x, new_caches[0], new_caches[1]

    return jax.shard_map(local_step, mesh=mesh, in_specs=in_specs, out_specs=out_specs, check_vma=False)
```

time: 300 us -> 91.6 us (0.31)
  waiting for transfers between devices: 139 us -> 0 us
  Pallas kernels: 0 us -> 89.1 us
  matrix products: 61 us -> 0 us
  blocking collectives: 37.2 us -> 0 us
  other arithmetic: 28.2 us -> 0 us
  local copies, waits for them, and re-layouts: 18.9 us -> 1.57 us
  between operations: 14.2 us -> 0.66 us
    psum x4 -> x0, waiting for transfers between devices: 139 us -> none  [the longest x2 73 us: local_step(): attn_out = lax.psum(attn_part, 'tp')]
    pallas_call x0 -> x4, Pallas kernels: none -> 89.1 us  [the longest x2 59.7 us: ffn_call(): pl.pallas_call(functools.partial(ffn_kernel, layer, n_tp, n_dp), out_shap...]
    dot_general x20 -> x0, matrix products: 61 us -> none  [the longest x2 13.2 us: local_step(): jnp.dot(hidden, down_rows, preferred_element_type=jnp.float32)]
    all_to_all x2 -> x0, blocking collectives: 22.4 us -> none  [local_step(): received = lax.all_to_all(ffn_partial, 'dp', 0, 0, tiled=True)]
    all_gather x2 -> x0, blocking collectives: 14.8 us -> none  [local_step(): all_in = lax.all_gather(ffn_in, 'dp', axis=0, tiled=True)]
    select_n x2 -> x0, other arithmetic: 12.8 us -> none  [attention_local(): new_cache = jnp.where(is_slot, new_entry[:, None, :], cache)]
    dot_general x3 -> x0, local copies, waits for them, and re-layouts: 8.16 us -> none  [attention_local(): jnp.dot(q_low, w_qb, preferred_element_type=jnp.float32)]
    reduce_sum x8 -> x0, other arithmetic: 6.13 us -> none  [the longest x6 4.58 us: rms_norm(): jnp.mean(wide_vals * wide_vals, axis=-1, keepdims=True) + NORM_EPS]
  transfers between devices with their start and end apart: 4 -> 0, of which waited for: 4 -> 0; matrix products, arithmetic and copies ran while one was open for 1% -> 0% of each run, Pallas kernels for 0% -> 0%
where the time goes in v1:
time: 91.6 us; the launch traced here: 91.4 us
  Pallas kernels  89.1 us (97%)
  local copies, waits for them, and re-layouts  1.57 us (2%)
    pallas_call x2, Pallas kernels, ffn_call(): pl.pallas_call(functools.partial(ffn_kernel, layer, n_tp, n_dp), out_shap...  59.7 us
    pallas_call x2, Pallas kernels, attn_call(): pl.pallas_call(functools.partial(attn_kernel, layer), out_shape=(jax.Shap...  29.5 us

profile of v1, /device:TPU:0, one launch (start us, length us, event | category | flops | bytes accessed | tf_op | source)
XLA Modules:
  0.0 91.4 jit_solution(15353958876897765591)
XLA Ops:
  0.6 14.7 %attn0.1 = (f32[32,2048]{1,0:T(8,128)}, bf16[32,576,256]{2,1,0:T(8,128)(2,1)}) custom-call(bf16[32,2048]{1,0:T(8,128)(2,1)} %x_ref.1, s32[32]{0:T(128)} %len_s.3, s32[1,32]{1,0:T(1,128)} %bitcast.20, f32[2,2048]{1,0:T(2,128)} %ag_ref.3, f32[2,512]{1,0:T(2,128)} %kg_ref.3, f32[2,1536]{1,0:T(2,128)} %qg_ref.3, bf16[32,576,256]{2,1,0:T(8,128)(2,1)} %bitcast.13, ...), custom_call_target="tpu_custom_call" | custom-call | flops 2000000000 | bytes 33000000 | tf_op jit(solution)/shard_map/attn0/pallas_call | solution.py:167
  15.3 31.1 %ffn0.1.x_ref = bf16[4,8,2048]{2,1,0:T(8,128)(2,1)} custom-call(f32[4,8,2048]{2,1,0:T(8,128)} %bitcast.19, bf16[4,8,2048]{2,1,0:T(8,128)(2,1)} %bitcast.16, f32[2,2048]{1,0:T(2,128)} %fg_ref.3, bf16[2,2048,11264]{2,1,0:T(8,128)(2,1)} %w_gate.3, bf16[2,2048,11264]{2,1,0:T(8,128)(2,1)} %w_up.3, bf16[2,11264,2048]{2,1,0:T(8,128)(2,1)} %w_down.3), custom_call_target="tpu_custom_call" | custom-call | flops 1100000000 | bytes 35000000 | tf_op jit(solution)/shard_map/ffn0/pallas_call | solution.py:296
  46.5 14.8 %attn1.1 = (f32[32,2048]{1,0:T(8,128)}, bf16[32,576,256]{2,1,0:T(8,128)(2,1)}) custom-call(bf16[32,2048]{1,0:T(8,128)(2,1)} %bitcast.15, s32[32]{0:T(128)} %len_s.3, s32[1,32]{1,0:T(1,128)} %bitcast.21, f32[2,2048]{1,0:T(2,128)} %ag_ref.3, f32[2,512]{1,0:T(2,128)} %kg_ref.3, f32[2,1536]{1,0:T(2,128)} %qg_ref.3, bf16[32,576,256]{2,1,0:T(8,128)(2,1)} %bitcast.14, ...), custom_call_target="tpu_custom_call" | custom-call | flops 2000000000 | bytes 33000000 | tf_op jit(solution)/shard_map/attn1/pallas_call | solution.py:167
  61.3 28.5 %ffn1.1 = bf16[4,8,2048]{2,1,0:T(8,128)(2,1)} custom-call(f32[4,8,2048]{2,1,0:T(8,128)} %bitcast.18, bf16[4,8,2048]{2,1,0:T(8,128)(2,1)} %ffn0.1.x_ref, f32[2,2048]{1,0:T(2,128)} %fg_ref.3, bf16[2,2048,11264]{2,1,0:T(8,128)(2,1)} %w_gate.3, bf16[2,2048,11264]{2,1,0:T(8,128)(2,1)} %w_up.3, bf16[2,11264,2048]{2,1,0:T(8,128)(2,1)} %w_down.3), custom_call_target="tpu_custom_call" | custom-call | flops 1100000000 | bytes 35000000 | tf_op jit(solution)/shard_map/ffn1/pallas_call | solution.py:296
  89.8 1.6 %copy.21 = bf16[32,2048]{1,0:T(8,128)(2,1)} copy(bf16[32,2048]{1,0:T(8,128)(2,1)} %bitcast.17) | data formatting | bytes 262144

commit v2 on v1

--- a/solution.py
+++ b/solution.py
@@ -26,7 +26,7 @@
 
 
 def attn_kernel(layer, x_ref, len_s, len_v, ag_ref, kg_ref, qg_ref, cache, w_dkv, w_qa, w_qb, w_uk, w_uv, w_o, part_ref, out_cache,
-                c_v, dkv_v, qa_v, qb_v, uk_v, uv_v, o_v, qlow_s, ent_s, qs, qb16, sc_s, p_s, os, ho_s, wsem, csem, osem):
+                c_v, c_new, dkv_v, qa_v, qb_v, uk_v, uv_v, o_v, qlow_s, ent_f, qs, qb16, sc_s, p_s, os, ho_s, wsem, csem, osem):
     rows, lat, rope, heads, qk = 32, 512, 64, 4, 192
     slots = c_v.shape[2]
     per = 4
@@ -46,7 +46,7 @@
         return pltpu.make_async_copy(cache.at[pl.ds(g * per, per)], c_v.at[pl.ds(g * per, per)], csem.at[g])
 
     def cache_out(g):
-        return pltpu.make_async_copy(c_v.at[pl.ds(g * per, per)], out_cache.at[pl.ds(g * per, per)], osem.at[g])
+        return pltpu.make_async_copy(c_new.at[pl.ds(g * per, per)], out_cache.at[pl.ds(g * per, per)], osem.at[g])
 
     for n in range(qa_n + 3):
         copies[n].start()
@@ -73,14 +73,15 @@
     for g in range(2, groups):
         cache_in(g).start()
     copies[qa_n].wait()
-    kt = lax.dot_general(dkv_v[...], h, NT, preferred_element_type=F32)
+    cut = (lat + rope) // 2
+    kt = jnp.concatenate([lax.dot_general(dkv_v[0:cut], h, NT, preferred_element_type=F32), lax.dot_general(dkv_v[cut:], h, NT, preferred_element_type=F32)], axis=0)
     kl = kt[:lat]
     inv_k = lax.rsqrt(jnp.mean(kl * kl, axis=0, keepdims=True) + EPS)
     gain_t = jnp.broadcast_to(kg_ref[layer:layer + 1, :], (128, lat)).T[:, :rows]
-    ent_s[0:lat, 0:rows] = (kl * inv_k * gain_t).astype(BF16).astype(F32)
+    ent_f[0:lat, 0:rows] = (kl * inv_k * gain_t).astype(BF16).astype(F32)
     ka, kb = kt[lat:lat + half], kt[lat + half:]
-    ent_s[lat:lat + half, 0:rows] = (ka * cos_t - kb * sin_t).astype(BF16).astype(F32)
-    ent_s[lat + half:, 0:rows] = (kb * cos_t + ka * sin_t).astype(BF16).astype(F32)
+    ent_f[lat:lat + half, 0:rows] = (ka * cos_t - kb * sin_t).astype(BF16).astype(F32)
+    ent_f[lat + half:, 0:rows] = (kb * cos_t + ka * sin_t).astype(BF16).astype(F32)
 
     inv_q = lax.rsqrt(ssq / (qa_n * width) + EPS)
     copies[qa_n + 1].wait()
@@ -101,51 +102,57 @@
     copies[qa_n + 4].start()
 
     lane = lax.broadcasted_iota(jnp.int32, (1, slots), 1)
-    lane_full = lax.broadcasted_iota(jnp.int32, (per * heads, slots), 1)
-    row_of = lax.broadcasted_iota(jnp.int32, (per * heads, 1), 0) // heads
     row_w = lax.broadcasted_iota(jnp.int32, (per * heads, slots), 0) // heads
     row_l = lax.broadcasted_iota(jnp.int32, (per * heads, lat), 0) // heads
     scale = float(qk) ** -0.5
 
-    def score_group(g):
-        q16 = qb16[pl.ds(pl.multiple_of(g * 16, 16), 16), 0:lat + rope]
-        ent = ent_s[...]
+    def insert(g):
+        for i in range(per):
+            r = g * per + i
+            col = jnp.broadcast_to(ent_f[:, r:r + 1], (lat + rope, 128)).astype(BF16)
+            hit = jnp.broadcast_to(lane == len_s[r], (lat + rope, slots))
+            c_new[r] = jnp.where(hit, jnp.concatenate([col, col], axis=-1), c_v[r])
+        cache_out(g).start()
+
+    for g in range(groups):
+        if g % 2 == 0:
+            cache_in(g).wait()
+            cache_in(g + 1).wait()
+        q16 = qb16[g * 16:(g + 1) * 16, 0:lat + rope]
         acc = None
         for i in range(per):
-            r = g * per + i
-            n_r = len_s[r]
-            col = jnp.broadcast_to(ent[:, i:i + 1], (lat + rope, slots)).astype(BF16)
-            hit = jnp.broadcast_to(lane == n_r, (lat + rope, slots))
-            new = jnp.where(hit, col, c_v[r])
-            c_v[r] = new
-            s_i = mm(q16, new) * scale
-            s_i = jnp.where(lane_full <= n_r, s_i, -1e30)
+            s_i = mm(q16, c_v[g * per + i])
             acc = s_i if acc is None else jnp.where(row_w == i, s_i, acc)
-        ent_s[...] = pltpu.roll(ent, 128 - per, 1)
-        sc_s[pl.ds(pl.multiple_of(g * 16, 16), 16), :] = acc
-
-    def score_loop(g, c):
-        cache_in(g).wait()
-        score_group(g)
-        cache_out(g).start()
-        return c
-
-    lax.fori_loop(0, groups, score_loop, 0)
-    s = sc_s[...]
-    e = jnp.exp(s - jnp.max(s, axis=-1, keepdims=True))
-    p_s[...] = (e / jnp.sum(e, axis=-1, keepdims=True)).astype(BF16)
-
-    def out_loop(g, c):
-        p16 = p_s[pl.ds(pl.multiple_of(g * 16, 16), 16), :]
+        sc_s[g * 16:(g + 1) * 16, :] = acc
+        if g % 2 == 0:
+            insert(g)
+    pairs = rows * heads
+    mine = lax.broadcasted_iota(jnp.int32, (pairs, rows), 0) // heads == lax.broadcasted_iota(jnp.int32, (pairs, rows), 1)
+    ent = ent_f[:, 0:rows].astype(BF16)
+    s_new = jnp.sum(jnp.where(mine, mm(qb16[:, 0:lat + rope], ent), 0.0), axis=-1, keepdims=True) * scale
+    len_p = jnp.sum(jnp.where(mine, jnp.broadcast_to(lens_row, (pairs, rows)), 0.0), axis=-1, keepdims=True)
+    lane_p = lax.broadcasted_iota(jnp.int32, (pairs, slots), 1).astype(F32)
+    s = jnp.where(lane_p < len_p, sc_s[...] * scale, -1e30)
+    top = jnp.maximum(jnp.max(s, axis=-1, keepdims=True), s_new)
+    e = jnp.exp(s - top)
+    e_new = jnp.exp(s_new - top)
+    total = jnp.sum(e, axis=-1, keepdims=True) + e_new
+    p_s[...] = jnp.where(lane_p < len_p, e / total, 0.0).astype(BF16)
+    p_new = jnp.where(mine, jnp.broadcast_to(e_new / total, (pairs, rows)), 0.0).astype(BF16)
+    o_new = lax.dot_general(p_new, ent[0:lat], NT, preferred_element_type=F32)
+    for c in range(lat // 128):
+        os[c] = o_new[:, c * 128:(c + 1) * 128]
+
+    for g in range(groups):
+        p16 = p_s[g * 16:(g + 1) * 16, :]
         acc = None
         for i in range(per):
             o_i = lax.dot_general(p16, c_v[g * per + i, 0:lat, :], NT, preferred_element_type=F32)
             acc = o_i if acc is None else jnp.where(row_l == i, o_i, acc)
         for c in range(lat // 128):
-            os[c, pl.ds(pl.multiple_of(g * 16, 16), 16), :] = acc[:, c * 128:(c + 1) * 128]
-        return c
-
-    lax.fori_loop(0, groups, out_loop, 0)
+            os[c, g * 16:(g + 1) * 16, :] += acc[:, c * 128:(c + 1) * 128]
+        if g % 2 == 1:
+            insert(g)
     copies[qa_n + 3].wait()
     for hd in range(heads):
         o_lat = jnp.concatenate([os[c, pl.ds(hd, rows, stride=heads), :].astype(BF16) for c in range(lat // 128)], axis=-1)
@@ -170,6 +177,7 @@
         in_specs=[vmem, smem, vmem, vmem, vmem, vmem] + [any_spec] * 7,
         out_specs=(vmem, any_spec),
         scratch_shapes=[
+            pltpu.VMEM(cache_t.shape, BF16),
             pltpu.VMEM(cache_t.shape, BF16),
             pltpu.VMEM(w_dkv_t.shape[1:], BF16),
             pltpu.VMEM(w_qa.shape[1:], BF16),
@@ -195,23 +203,11 @@
     )(x, lengths, lengths.reshape(1, rows), attn_gain, kv_gain, q_gain, cache_t, w_dkv_t, w_qa, w_qb, w_uk, w_uv, w_o)
 
 
-def ffn_kernel(layer, n_tp, n_dp, part_ref, x_ref, fg_ref, w_gate, w_up, w_down, out_ref,
-               g_v, u_v, d_v, rs_buf, xm_s, g_snd, g_buf, hid, f_snd, f_buf, x_snd,
-               wsem, s_rs, r_rs, s_g, r_g, s_f, r_f, s_x, r_x):
+def ffn_kernel(layer, n_tp, n_dp, part, x, gain, w_gate, w_up, w_down, out_ref,
+               part_v, x_v, gain_v, g_v, u_v, d_v, rs_buf, xm_s, g_all, hid, f_snd, f_buf, x_snd,
+               isem, wsem, s_rs, r_rs, s_g, r_g, s_f, r_f, s_x, r_x):
     z = lax.axis_index("tp")
     d = lax.axis_index("dp")
-    hid_w = g_v.shape[1]
-    start = pl.multiple_of(d * hid_w, hid_w)
-    half = hid_w // 2
-    loads = []
-    for c in range(2):
-        loads.append(pltpu.make_async_copy(w_gate.at[layer, :, pl.ds(pl.multiple_of(start + c * half, 128), half)], g_v.at[:, pl.ds(c * half, half)], wsem.at[3 * c]))
-        loads.append(pltpu.make_async_copy(w_up.at[layer, :, pl.ds(pl.multiple_of(start + c * half, 128), half)], u_v.at[:, pl.ds(c * half, half)], wsem.at[3 * c + 1]))
-    for c in range(2):
-        loads.append(pltpu.make_async_copy(w_down.at[layer, pl.ds(start + c * half, half), :], d_v.at[pl.ds(c * half, half), :], wsem.at[3 * c + 2]))
-    for cp in loads:
-        cp.start()
-
     tp_peers = [lax.rem(z + k, n_tp) for k in range(1, n_tp)]
     dp_peers = [lax.rem(d + k, n_dp) for k in range(1, n_dp)]
     barrier = pltpu.get_barrier_semaphore()
@@ -219,32 +215,56 @@
         pl.semaphore_signal(barrier, inc=1, device_id={"tp": pz}, device_id_type=MESH)
     for pd in dp_peers:
         pl.semaphore_signal(barrier, inc=1, device_id={"dp": pd}, device_id_type=MESH)
+
+    ins = [pltpu.make_async_copy(part, part_v, isem.at[0]), pltpu.make_async_copy(x.at[z], x_v, isem.at[1]), pltpu.make_async_copy(gain, gain_v, isem.at[2])]
+    for cp in ins:
+        cp.start()
+    hid_w = g_v.shape[1]
+    start = pl.multiple_of(d * hid_w, hid_w)
+    half = hid_w // 2
+    loads = []
+    for c in range(2):
+        cols = pl.ds(pl.multiple_of(start + c * half, 128), half)
+        loads.append(pltpu.make_async_copy(w_gate.at[layer, :, cols], g_v.at[:, pl.ds(c * half, half)], wsem.at[2 * c]))
+        loads.append(pltpu.make_async_copy(w_up.at[layer, :, cols], u_v.at[:, pl.ds(c * half, half)], wsem.at[2 * c + 1]))
+    for c in range(2):
+        loads.append(pltpu.make_async_copy(w_down.at[layer, pl.ds(start + c * half, half), :], d_v.at[pl.ds(c * half, half), :], wsem.at[4 + c]))
+    for cp in loads:
+        cp.start()
+
+    dim = x_v.shape[1]
+    own = x_v.shape[0]
+    chunks = 4
+    wide = dim // chunks
+
+    def send(axis, peer, src, dst, ssem, rsem, i):
+        cp = pltpu.make_async_remote_copy(src_ref=src, dst_ref=dst, send_sem=ssem.at[i], recv_sem=rsem.at[i], device_id={axis: peer}, device_id_type=MESH)
+        cp.start()
+        return cp
+
     pl.semaphore_wait(barrier, n_tp + n_dp - 2)
-
-    def exchange(peers, axis, src_of, dst_of, ssem, rsem):
-        cps = []
-        for k, p in enumerate(peers):
-            cps.append(pltpu.make_async_remote_copy(src_ref=src_of(k, p), dst_ref=dst_of(k), send_sem=ssem.at[k], recv_sem=rsem.at[k], device_id={axis: p}, device_id_type=MESH))
-        return cps
-
-    rs = exchange(tp_peers, "tp", lambda k, p: part_ref.at[p], lambda k: rs_buf.at[k], s_rs, r_rs)
-    for cp in rs:
-        cp.start()
-    acc = x_ref[z].astype(F32)
-    tot = part_ref[z]
-    for k, cp in enumerate(rs):
-        cp.wait_recv()
-        tot = tot + rs_buf[k]
-    xm = (acc + tot).astype(BF16).astype(F32)
-    xm_s[...] = xm
-    g = rms(xm, fg_ref[layer:layer + 1, :])
-    g_snd[...] = g
-    gx = exchange(dp_peers, "dp", lambda k, p: g_snd, lambda k: g_buf.at[k], s_g, r_g)
-    for cp in gx:
-        cp.start()
+    for cp in ins:
+        cp.wait()
+    rs, gx, fx, xx = [], [], [], []
+    for c in range(chunks):
+        cols = pl.ds(c * wide, wide)
+        for k, p in enumerate(tp_peers):
+            rs.append(send("tp", p, part_v.at[p, :, cols], rs_buf.at[k, :, cols], s_rs, r_rs, c * (n_tp - 1) + k))
+    for c in range(chunks):
+        cols = slice(c * wide, (c + 1) * wide)
+        tot = part_v[z, :, cols]
+        for k in range(n_tp - 1):
+            rs[c * (n_tp - 1) + k].wait_recv()
+            tot = tot + rs_buf[k, :, cols]
+        xm = (x_v[:, cols].astype(F32) + tot).astype(BF16)
+        xm_s[:, cols] = xm.astype(F32)
+        g_all[0, :, cols] = xm
+        for k, p in enumerate(dp_peers):
+            gx.append(send("dp", p, g_all.at[0, :, pl.ds(c * wide, wide)], g_all.at[k + 1, :, pl.ds(c * wide, wide)], s_g, r_g, c * (n_dp - 1) + k))
     for cp in gx:
         cp.wait_recv()
-    full = jnp.concatenate([g.astype(F32)] + [g_buf[k].astype(F32) for k in range(n_dp - 1)], axis=0).astype(BF16)
+    mids = jnp.concatenate([g_all[k].astype(F32) for k in range(n_dp)], axis=0)
+    full = rms(mids, gain_v[layer:layer + 1, :])
 
     tile = 256
     for j in range(hid_w // tile):
@@ -260,26 +280,24 @@
     loads[4].wait()
     loads[5].wait()
     hv = hid[...]
-    own = []
-    for j in range(4):
-        y = mm(hv, d_v[:, j * 512:(j + 1) * 512])
-        for k in range(n_dp):
-            f_snd[k, :, j * 512:(j + 1) * 512] = y[k * 8:(k + 1) * 8].astype(BF16)
-    fx = []
-    for k, p in enumerate(dp_peers):
-        fx.append(pltpu.make_async_remote_copy(src_ref=f_snd.at[n_dp - 1 - k], dst_ref=f_buf.at[k], send_sem=s_f.at[k], recv_sem=r_f.at[k], device_id={"dp": p}, device_id_type=MESH))
-    for cp in fx:
-        cp.start()
-    tot = f_snd[0].astype(F32)
-    for k, cp in enumerate(fx):
-        cp.wait_recv()
-        tot = tot + f_buf[k].astype(F32)
-    x_new = (xm_s[...] + tot).astype(BF16)
-    x_snd[...] = x_new
-    out_ref[z] = x_new
-    xx = exchange(tp_peers, "tp", lambda k, p: x_snd, lambda k: out_ref.at[z], s_x, r_x)
-    for cp in xx:
-        cp.start()
+    for c in range(chunks):
+        y = mm(hv, d_v[:, c * wide:(c + 1) * wide])
+        for b in range(n_dp):
+            f_snd[b, :, c * wide:(c + 1) * wide] = y[b * own:(b + 1) * own].astype(BF16)
+        cols = pl.ds(c * wide, wide)
+        for k, p in enumerate(dp_peers):
+            fx.append(send("dp", p, f_snd.at[n_dp - 1 - k, :, cols], f_buf.at[k, :, cols], s_f, r_f, c * (n_dp - 1) + k))
+    for c in range(chunks):
+        cols = slice(c * wide, (c + 1) * wide)
+        tot = f_snd[0, :, cols].astype(F32)
+        for k in range(n_dp - 1):
+            fx[c * (n_dp - 1) + k].wait_recv()
+            tot = tot + f_buf[k, :, cols].astype(F32)
+        x_new = (xm_s[:, cols] + tot).astype(BF16)
+        x_snd[:, cols] = x_new
+        out_ref[z, :, cols] = x_new
+        for k, p in enumerate(tp_peers):
+            xx.append(send("tp", p, x_snd.at[:, pl.ds(c * wide, wide)], out_ref.at[z, :, pl.ds(c * wide, wide)], s_x, r_x, c * (n_tp - 1) + k))
     for cp in xx:
         cp.wait_recv()
     for cp in rs + gx + fx + xx:
@@ -293,24 +311,27 @@
     own = rows // n_tp
     hid_w = w_gate.shape[2] // n_dp
     dma = pltpu.SemaphoreType.DMA
+    sends = dma((4 * (n_tp - 1),))
     out = pl.pallas_call(
         functools.partial(ffn_kernel, layer, n_tp, n_dp),
         out_shape=jax.ShapeDtypeStruct((n_tp, own, dim), BF16),
-        in_specs=[vmem, vmem, vmem] + [any_spec] * 3,
+        in_specs=[any_spec] * 6,
         out_specs=vmem,
         scratch_shapes=[
+            pltpu.VMEM((n_tp, own, dim), F32),
+            pltpu.VMEM((own, dim), BF16),
+            pltpu.VMEM(ffn_gain.shape, F32),
             pltpu.VMEM((dim, hid_w), BF16),
             pltpu.VMEM((dim, hid_w), BF16),
             pltpu.VMEM((hid_w, dim), BF16),
             pltpu.VMEM((n_tp - 1, own, dim), F32),
             pltpu.VMEM((own, dim), F32),
-            pltpu.VMEM((own, dim), BF16),
-            pltpu.VMEM((n_dp - 1, own, dim), BF16),
+            pltpu.VMEM((n_dp, own, dim), BF16),
             pltpu.VMEM((own * n_dp, hid_w), BF16),
             pltpu.VMEM((n_dp, own, dim), BF16),
             pltpu.VMEM((n_dp - 1, own, dim), BF16),
             pltpu.VMEM((own, dim), BF16),
-            dma((6,)), dma((3,)), dma((3,)), dma((3,)), dma((3,)), dma((3,)), dma((3,)), dma((3,)), dma((3,)),
+            dma((3,)), dma((6,)), sends, sends, sends, sends, sends, sends, sends, sends,
         ],
         compiler_params=pltpu.CompilerParams(vmem_limit_bytes=VMEM_LIMIT, collective_id=layer, has_side_effects=True),
         cost_estimate=pl.CostEstimate(flops=1_100_000_000, bytes_accessed=35_000_000, transcendentals=0),

time: 91.6 us -> 102 us (1.11)
  Pallas kernels: 89.1 us -> 99.1 us
    pallas_call x2, Pallas kernels: 59.7 us -> 70.2 us  [ffn_call(): pl.pallas_call(functools.partial(ffn_kernel, layer, n_tp, n_dp), out_shap...]
where the time goes in v2:
time: 102 us; the launch traced here: 101 us
  Pallas kernels  99.1 us (97%)
  local copies, waits for them, and re-layouts  1.57 us (2%)
    pallas_call x2, Pallas kernels, ffn_call(): pl.pallas_call(functools.partial(ffn_kernel, layer, n_tp, n_dp), out_shap...  70.2 us
    pallas_call x2, Pallas kernels, attn_call(): pl.pallas_call(functools.partial(attn_kernel, layer), out_shape=(jax.Shap...  28.9 us

profile of v2, /device:TPU:0, one launch (start us, length us, event | category | flops | bytes accessed | tf_op | source)
XLA Modules:
  0.0 101.3 jit_solution(1538069587738004931)
XLA Ops:
  0.6 14.6 %attn0.1 = (f32[32,2048]{1,0:T(8,128)}, bf16[32,576,256]{2,1,0:T(8,128)(2,1)}) custom-call(bf16[32,2048]{1,0:T(8,128)(2,1)} %x_ref.1, s32[32]{0:T(128)} %len_s.3, s32[1,32]{1,0:T(1,128)} %bitcast.20, f32[2,2048]{1,0:T(2,128)} %ag_ref.3, f32[2,512]{1,0:T(2,128)} %kg_ref.3, f32[2,1536]{1,0:T(2,128)} %qg_ref.3, bf16[32,576,256]{2,1,0:T(8,128)(2,1)} %bitcast.13, ...), custom_call_target="tpu_custom_call" | custom-call | flops 2000000000 | bytes 33000000 | tf_op jit(solution)/shard_map/attn0/pallas_call | solution.py:174
  15.3 35.7 %ffn0.1.x = bf16[4,8,2048]{2,1,0:T(8,128)(2,1)} custom-call(f32[4,8,2048]{2,1,0:T(8,128)} %bitcast.19, bf16[4,8,2048]{2,1,0:T(8,128)(2,1)} %bitcast.16, f32[2,2048]{1,0:T(2,128)} %gain.3, bf16[2,2048,11264]{2,1,0:T(8,128)(2,1)} %w_gate.3, bf16[2,2048,11264]{2,1,0:T(8,128)(2,1)} %w_up.3, bf16[2,11264,2048]{2,1,0:T(8,128)(2,1)} %w_down.3), custom_call_target="tpu_custom_call" | custom-call | flops 1100000000 | bytes 35000000 | tf_op jit(solution)/shard_map/ffn0/pallas_call | solution.py:315
  51.0 14.3 %attn1.1 = (f32[32,2048]{1,0:T(8,128)}, bf16[32,576,256]{2,1,0:T(8,128)(2,1)}) custom-call(bf16[32,2048]{1,0:T(8,128)(2,1)} %bitcast.15, s32[32]{0:T(128)} %len_s.3, s32[1,32]{1,0:T(1,128)} %bitcast.21, f32[2,2048]{1,0:T(2,128)} %ag_ref.3, f32[2,512]{1,0:T(2,128)} %kg_ref.3, f32[2,1536]{1,0:T(2,128)} %qg_ref.3, bf16[32,576,256]{2,1,0:T(8,128)(2,1)} %bitcast.14, ...), custom_call_target="tpu_custom_call" | custom-call | flops 2000000000 | bytes 33000000 | tf_op jit(solution)/shard_map/attn1/pallas_call | solution.py:174
  65.3 34.5 %ffn1.1 = bf16[4,8,2048]{2,1,0:T(8,128)(2,1)} custom-call(f32[4,8,2048]{2,1,0:T(8,128)} %bitcast.18, bf16[4,8,2048]{2,1,0:T(8,128)(2,1)} %ffn0.1.x, f32[2,2048]{1,0:T(2,128)} %gain.3, bf16[2,2048,11264]{2,1,0:T(8,128)(2,1)} %w_gate.3, bf16[2,2048,11264]{2,1,0:T(8,128)(2,1)} %w_up.3, bf16[2,11264,2048]{2,1,0:T(8,128)(2,1)} %w_down.3), custom_call_target="tpu_custom_call" | custom-call | flops 1100000000 | bytes 35000000 | tf_op jit(solution)/shard_map/ffn1/pallas_call | solution.py:315
  99.8 1.6 %copy.21 = bf16[32,2048]{1,0:T(8,128)(2,1)} copy(bf16[32,2048]{1,0:T(8,128)(2,1)} %bitcast.17) | data formatting | bytes 262144

commit v3 on v2

--- a/solution.py
+++ b/solution.py
@@ -221,16 +221,16 @@
         cp.start()
     hid_w = g_v.shape[1]
     start = pl.multiple_of(d * hid_w, hid_w)
-    half = hid_w // 2
-    loads = []
-    for c in range(2):
-        cols = pl.ds(pl.multiple_of(start + c * half, 128), half)
-        loads.append(pltpu.make_async_copy(w_gate.at[layer, :, cols], g_v.at[:, pl.ds(c * half, half)], wsem.at[2 * c]))
-        loads.append(pltpu.make_async_copy(w_up.at[layer, :, cols], u_v.at[:, pl.ds(c * half, half)], wsem.at[2 * c + 1]))
-    for c in range(2):
-        loads.append(pltpu.make_async_copy(w_down.at[layer, pl.ds(start + c * half, half), :], d_v.at[pl.ds(c * half, half), :], wsem.at[4 + c]))
-    for cp in loads:
-        cp.start()
+    quarter = g_v.shape[0] // 4
+    wide_loads, down_loads = [], []
+    for c in range(4):
+        rows = pl.ds(c * quarter, quarter)
+        wide_loads.append(pltpu.make_async_copy(w_gate.at[layer, rows, pl.ds(start, hid_w)], g_v.at[rows, :], wsem.at[c]))
+        wide_loads.append(pltpu.make_async_copy(w_up.at[layer, rows, pl.ds(start, hid_w)], u_v.at[rows, :], wsem.at[4 + c]))
+    for c in range(4):
+        rows = hid_w // 4
+        down_loads.append(pltpu.make_async_copy(w_down.at[layer, pl.ds(start + c * rows, rows), :], d_v.at[pl.ds(c * rows, rows), :], wsem.at[8 + c]))
+    wide_loads[0].start()
 
     dim = x_v.shape[1]
     own = x_v.shape[0]
@@ -250,6 +250,8 @@
         cols = pl.ds(c * wide, wide)
         for k, p in enumerate(tp_peers):
             rs.append(send("tp", p, part_v.at[p, :, cols], rs_buf.at[k, :, cols], s_rs, r_rs, c * (n_tp - 1) + k))
+    for cp in wide_loads[1:5]:
+        cp.start()
     for c in range(chunks):
         cols = slice(c * wide, (c + 1) * wide)
         tot = part_v[z, :, cols]
@@ -261,24 +263,24 @@
         g_all[0, :, cols] = xm
         for k, p in enumerate(dp_peers):
             gx.append(send("dp", p, g_all.at[0, :, pl.ds(c * wide, wide)], g_all.at[k + 1, :, pl.ds(c * wide, wide)], s_g, r_g, c * (n_dp - 1) + k))
+        if c < 3:
+            wide_loads[5 + c].start()
+    for cp in down_loads:
+        cp.start()
     for cp in gx:
         cp.wait_recv()
     mids = jnp.concatenate([g_all[k].astype(F32) for k in range(n_dp)], axis=0)
     full = rms(mids, gain_v[layer:layer + 1, :])
 
+    for cp in wide_loads:
+        cp.wait()
     tile = 256
     for j in range(hid_w // tile):
-        if j == 0:
-            loads[0].wait()
-            loads[1].wait()
-        if (j + 1) * tile > half and j * tile <= half:
-            loads[2].wait()
-            loads[3].wait()
         gate = mm(full, g_v[:, j * tile:(j + 1) * tile])
         up = mm(full, u_v[:, j * tile:(j + 1) * tile])
         hid[:, j * tile:(j + 1) * tile] = (gate * jax.nn.sigmoid(gate) * up).astype(BF16)
-    loads[4].wait()
-    loads[5].wait()
+    for cp in down_loads:
+        cp.wait()
     hv = hid[...]
     for c in range(chunks):
         y = mm(hv, d_v[:, c * wide:(c + 1) * wide])
@@ -331,7 +333,7 @@
             pltpu.VMEM((n_dp, own, dim), BF16),
             pltpu.VMEM((n_dp - 1, own, dim), BF16),
             pltpu.VMEM((own, dim), BF16),
-            dma((3,)), dma((6,)), sends, sends, sends, sends, sends, sends, sends, sends,
+            dma((3,)), dma((12,)), sends, sends, sends, sends, sends, sends, sends, sends,
         ],
         compiler_params=pltpu.CompilerParams(vmem_limit_bytes=VMEM_LIMIT, collective_id=layer, has_side_effects=True),
         cost_estimate=pl.CostEstimate(flops=1_100_000_000, bytes_accessed=35_000_000, transcendentals=0),

time: 102 us -> 87.4 us (0.86)
  Pallas kernels: 99.1 us -> 85 us
    pallas_call x2, Pallas kernels: 70.2 us -> 56 us  [ffn_call(): pl.pallas_call(functools.partial(ffn_kernel, layer, n_tp, n_dp), out_shap...]
where the time goes in v3:
time: 87.4 us; the launch traced here: 87.2 us
  Pallas kernels  85 us (97%)
  local copies, waits for them, and re-layouts  1.57 us (2%)
    pallas_call x2, Pallas kernels, ffn_call(): pl.pallas_call(functools.partial(ffn_kernel, layer, n_tp, n_dp), out_shap...  56 us
    pallas_call x2, Pallas kernels, attn_call(): pl.pallas_call(functools.partial(attn_kernel, layer), out_shape=(jax.Shap...  28.9 us

profile of v3, /device:TPU:0, one launch (start us, length us, event | category | flops | bytes accessed | tf_op | source)
XLA Modules:
  0.0 87.2 jit_solution(15469817492586856395)
XLA Ops:
  0.6 14.6 %attn0.1 = (f32[32,2048]{1,0:T(8,128)}, bf16[32,576,256]{2,1,0:T(8,128)(2,1)}) custom-call(bf16[32,2048]{1,0:T(8,128)(2,1)} %x_ref.1, s32[32]{0:T(128)} %len_s.3, s32[1,32]{1,0:T(1,128)} %bitcast.20, f32[2,2048]{1,0:T(2,128)} %ag_ref.3, f32[2,512]{1,0:T(2,128)} %kg_ref.3, f32[2,1536]{1,0:T(2,128)} %qg_ref.3, bf16[32,576,256]{2,1,0:T(8,128)(2,1)} %bitcast.13, ...), custom_call_target="tpu_custom_call" | custom-call | flops 2000000000 | bytes 33000000 | tf_op jit(solution)/shard_map/attn0/pallas_call | solution.py:174
  15.3 29.5 %ffn0.1.x = bf16[4,8,2048]{2,1,0:T(8,128)(2,1)} custom-call(f32[4,8,2048]{2,1,0:T(8,128)} %bitcast.19, bf16[4,8,2048]{2,1,0:T(8,128)(2,1)} %bitcast.16, f32[2,2048]{1,0:T(2,128)} %gain.3, bf16[2,2048,11264]{2,1,0:T(8,128)(2,1)} %w_gate.3, bf16[2,2048,11264]{2,1,0:T(8,128)(2,1)} %w_up.3, bf16[2,11264,2048]{2,1,0:T(8,128)(2,1)} %w_down.3), custom_call_target="tpu_custom_call" | custom-call | flops 1100000000 | bytes 35000000 | tf_op jit(solution)/shard_map/ffn0/pallas_call | solution.py:317
  44.8 14.3 %attn1.1 = (f32[32,2048]{1,0:T(8,128)}, bf16[32,576,256]{2,1,0:T(8,128)(2,1)}) custom-call(bf16[32,2048]{1,0:T(8,128)(2,1)} %bitcast.15, s32[32]{0:T(128)} %len_s.3, s32[1,32]{1,0:T(1,128)} %bitcast.21, f32[2,2048]{1,0:T(2,128)} %ag_ref.3, f32[2,512]{1,0:T(2,128)} %kg_ref.3, f32[2,1536]{1,0:T(2,128)} %qg_ref.3, bf16[32,576,256]{2,1,0:T(8,128)(2,1)} %bitcast.14, ...), custom_call_target="tpu_custom_call" | custom-call | flops 2000000000 | bytes 33000000 | tf_op jit(solution)/shard_map/attn1/pallas_call | solution.py:174
  59.1 26.5 %ffn1.1 = bf16[4,8,2048]{2,1,0:T(8,128)(2,1)} custom-call(f32[4,8,2048]{2,1,0:T(8,128)} %bitcast.18, bf16[4,8,2048]{2,1,0:T(8,128)(2,1)} %ffn0.1.x, f32[2,2048]{1,0:T(2,128)} %gain.3, bf16[2,2048,11264]{2,1,0:T(8,128)(2,1)} %w_gate.3, bf16[2,2048,11264]{2,1,0:T(8,128)(2,1)} %w_up.3, bf16[2,11264,2048]{2,1,0:T(8,128)(2,1)} %w_down.3), custom_call_target="tpu_custom_call" | custom-call | flops 1100000000 | bytes 35000000 | tf_op jit(solution)/shard_map/ffn1/pallas_call | solution.py:317
  85.6 1.6 %copy.21 = bf16[32,2048]{1,0:T(8,128)(2,1)} copy(bf16[32,2048]{1,0:T(8,128)(2,1)} %bitcast.17) | data formatting | bytes 262144

commit v4 on v3

--- a/solution.py
+++ b/solution.py
@@ -36,11 +36,8 @@
     copies = []
     for n in range(qa_n):
         copies.append(pltpu.make_async_copy(w_qa.at[layer, :, pl.ds(n * width, width)], qa_v.at[:, pl.ds(n * width, width)], wsem.at[n]))
-    copies.append(pltpu.make_async_copy(w_dkv.at[layer], dkv_v, wsem.at[qa_n]))
-    copies.append(pltpu.make_async_copy(w_qb.at[layer], qb_v, wsem.at[qa_n + 1]))
-    copies.append(pltpu.make_async_copy(w_uk.at[layer], uk_v, wsem.at[qa_n + 2]))
-    copies.append(pltpu.make_async_copy(w_uv.at[layer], uv_v, wsem.at[qa_n + 3]))
-    copies.append(pltpu.make_async_copy(w_o.at[layer], o_v, wsem.at[qa_n + 4]))
+    for i, (src, dst) in enumerate(((w_dkv, dkv_v), (w_qb, qb_v), (w_uk, uk_v), (w_uv, uv_v), (w_o, o_v))):
+        copies.append(pltpu.make_async_copy(src.at[layer], dst, wsem.at[qa_n + i]))
 
     def cache_in(g):
         return pltpu.make_async_copy(cache.at[pl.ds(g * per, per)], c_v.at[pl.ds(g * per, per)], csem.at[g])
@@ -48,8 +45,12 @@
     def cache_out(g):
         return pltpu.make_async_copy(c_new.at[pl.ds(g * per, per)], out_cache.at[pl.ds(g * per, per)], osem.at[g])
 
-    for n in range(qa_n + 3):
-        copies[n].start()
+    for cp in [copies[qa_n]] + copies[:qa_n] + copies[qa_n + 1:qa_n + 3]:
+        cp.start()
+    for g in range(groups):
+        cache_in(g).start()
+    copies[qa_n + 3].start()
+    copies[qa_n + 4].start()
 
     xf = x_ref[...].astype(F32)
     h = rms(xf, ag_ref[layer:layer + 1, :])
@@ -61,17 +62,6 @@
     cos_t, sin_t = jnp.cos(ang_t), jnp.sin(ang_t)
     cos_r, sin_r = cos_t.T, sin_t.T
 
-    ssq = jnp.zeros((rows, 1), F32)
-    for n in range(qa_n):
-        copies[n].wait()
-        if n == 0:
-            for g in range(2):
-                cache_in(g).start()
-        part = mm(h, qa_v[:, n * width:(n + 1) * width])
-        ssq = ssq + jnp.sum(part * part, axis=-1, keepdims=True)
-        qlow_s[:, n * width:(n + 1) * width] = part
-    for g in range(2, groups):
-        cache_in(g).start()
     copies[qa_n].wait()
     cut = (lat + rope) // 2
     kt = jnp.concatenate([lax.dot_general(dkv_v[0:cut], h, NT, preferred_element_type=F32), lax.dot_general(dkv_v[cut:], h, NT, preferred_element_type=F32)], axis=0)
@@ -83,6 +73,12 @@
     ent_f[lat:lat + half, 0:rows] = (ka * cos_t - kb * sin_t).astype(BF16).astype(F32)
     ent_f[lat + half:, 0:rows] = (kb * cos_t + ka * sin_t).astype(BF16).astype(F32)
 
+    ssq = jnp.zeros((rows, 1), F32)
+    for n in range(qa_n):
+        copies[n].wait()
+        part = mm(h, qa_v[:, n * width:(n + 1) * width])
+        ssq = ssq + jnp.sum(part * part, axis=-1, keepdims=True)
+        qlow_s[:, n * width:(n + 1) * width] = part
     inv_q = lax.rsqrt(ssq / (qa_n * width) + EPS)
     copies[qa_n + 1].wait()
     q_low = (qlow_s[...] * inv_q * qg_ref[layer:layer + 1, :]).astype(BF16)
@@ -98,8 +94,6 @@
         qs[lat // 128, pl.ds(hd, rows, stride=heads), :] = rot
     for c in range(lat // 128 + 1):
         qb16[:, c * 128:(c + 1) * 128] = qs[c].astype(BF16)
-    copies[qa_n + 3].start()
-    copies[qa_n + 4].start()
 
     lane = lax.broadcasted_iota(jnp.int32, (1, slots), 1)
     row_w = lax.broadcasted_iota(jnp.int32, (per * heads, slots), 0) // heads
@@ -124,8 +118,7 @@
             s_i = mm(q16, c_v[g * per + i])
             acc = s_i if acc is None else jnp.where(row_w == i, s_i, acc)
         sc_s[g * 16:(g + 1) * 16, :] = acc
-        if g % 2 == 0:
-            insert(g)
+        insert(g)
     pairs = rows * heads
     mine = lax.broadcasted_iota(jnp.int32, (pairs, rows), 0) // heads == lax.broadcasted_iota(jnp.int32, (pairs, rows), 1)
     ent = ent_f[:, 0:rows].astype(BF16)
@@ -151,8 +144,6 @@
             acc = o_i if acc is None else jnp.where(row_l == i, o_i, acc)
         for c in range(lat // 128):
             os[c, g * 16:(g + 1) * 16, :] += acc[:, c * 128:(c + 1) * 128]
-        if g % 2 == 1:
-            insert(g)
     copies[qa_n + 3].wait()
     for hd in range(heads):
         o_lat = jnp.concatenate([os[c, pl.ds(hd, rows, stride=heads), :].astype(BF16) for c in range(lat // 128)], axis=-1)
@@ -261,8 +252,10 @@
         xm = (x_v[:, cols].astype(F32) + tot).astype(BF16)
         xm_s[:, cols] = xm.astype(F32)
         g_all[0, :, cols] = xm
-        for k, p in enumerate(dp_peers):
-            gx.append(send("dp", p, g_all.at[0, :, pl.ds(c * wide, wide)], g_all.at[k + 1, :, pl.ds(c * wide, wide)], s_g, r_g, c * (n_dp - 1) + k))
+        if c % 2 == 1:
+            both = pl.ds((c - 1) * wide, 2 * wide)
+            for k, p in enumerate(dp_peers):
+                gx.append(send("dp", p, g_all.at[0, :, both], g_all.at[k + 1, :, both], s_g, r_g, c // 2 * (n_dp - 1) + k))
         if c < 3:
             wide_loads[5 + c].start()
     for cp in down_loads:
@@ -282,6 +275,7 @@
     for cp in down_loads:
         cp.wait()
     hv = hid[...]
+    chunks, wide = 2, dim // 2
     for c in range(chunks):
         y = mm(hv, d_v[:, c * wide:(c + 1) * wide])
         for b in range(n_dp):

time: 87.4 us -> 87.4 us (level)
  no operation moved by 1% of the time
where the time goes in v4:
time: 87.4 us; the launch traced here: 87.2 us
  Pallas kernels  85 us (97%)
  local copies, waits for them, and re-layouts  1.57 us (2%)
    pallas_call x2, Pallas kernels, ffn_call(): pl.pallas_call(functools.partial(ffn_kernel, layer, n_tp, n_dp), out_shap...  56.6 us
    pallas_call x2, Pallas kernels, attn_call(): pl.pallas_call(functools.partial(attn_kernel, layer), out_shape=(jax.Shap...  28.4 us

profile of v4, /device:TPU:0, one launch (start us, length us, event | category | flops | bytes accessed | tf_op | source)
XLA Modules:
  0.0 87.2 jit_solution(3644260087970350937)
XLA Ops:
  0.6 14.1 %attn0.1 = (f32[32,2048]{1,0:T(8,128)}, bf16[32,576,256]{2,1,0:T(8,128)(2,1)}) custom-call(bf16[32,2048]{1,0:T(8,128)(2,1)} %x_ref.1, s32[32]{0:T(128)} %len_s.3, s32[1,32]{1,0:T(1,128)} %bitcast.20, f32[2,2048]{1,0:T(2,128)} %ag_ref.3, f32[2,512]{1,0:T(2,128)} %kg_ref.3, f32[2,1536]{1,0:T(2,128)} %qg_ref.3, bf16[32,576,256]{2,1,0:T(8,128)(2,1)} %bitcast.13, ...), custom_call_target="tpu_custom_call" | custom-call | flops 2000000000 | bytes 33000000 | tf_op jit(solution)/shard_map/attn0/pallas_call | solution.py:165
  14.8 29.8 %ffn0.1.x = bf16[4,8,2048]{2,1,0:T(8,128)(2,1)} custom-call(f32[4,8,2048]{2,1,0:T(8,128)} %bitcast.19, bf16[4,8,2048]{2,1,0:T(8,128)(2,1)} %bitcast.16, f32[2,2048]{1,0:T(2,128)} %gain.3, bf16[2,2048,11264]{2,1,0:T(8,128)(2,1)} %w_gate.3, bf16[2,2048,11264]{2,1,0:T(8,128)(2,1)} %w_up.3, bf16[2,11264,2048]{2,1,0:T(8,128)(2,1)} %w_down.3), custom_call_target="tpu_custom_call" | custom-call | flops 1100000000 | bytes 35000000 | tf_op jit(solution)/shard_map/ffn0/pallas_call | solution.py:311
  44.6 14.3 %attn1.1 = (f32[32,2048]{1,0:T(8,128)}, bf16[32,576,256]{2,1,0:T(8,128)(2,1)}) custom-call(bf16[32,2048]{1,0:T(8,128)(2,1)} %bitcast.15, s32[32]{0:T(128)} %len_s.3, s32[1,32]{1,0:T(1,128)} %bitcast.21, f32[2,2048]{1,0:T(2,128)} %ag_ref.3, f32[2,512]{1,0:T(2,128)} %kg_ref.3, f32[2,1536]{1,0:T(2,128)} %qg_ref.3, bf16[32,576,256]{2,1,0:T(8,128)(2,1)} %bitcast.14, ...), custom_call_target="tpu_custom_call" | custom-call | flops 2000000000 | bytes 33000000 | tf_op jit(solution)/shard_map/attn1/pallas_call | solution.py:165
  58.9 26.8 %ffn1.1 = bf16[4,8,2048]{2,1,0:T(8,128)(2,1)} custom-call(f32[4,8,2048]{2,1,0:T(8,128)} %bitcast.18, bf16[4,8,2048]{2,1,0:T(8,128)(2,1)} %ffn0.1.x, f32[2,2048]{1,0:T(2,128)} %gain.3, bf16[2,2048,11264]{2,1,0:T(8,128)(2,1)} %w_gate.3, bf16[2,2048,11264]{2,1,0:T(8,128)(2,1)} %w_up.3, bf16[2,11264,2048]{2,1,0:T(8,128)(2,1)} %w_down.3), custom_call_target="tpu_custom_call" | custom-call | flops 1100000000 | bytes 35000000 | tf_op jit(solution)/shard_map/ffn1/pallas_call | solution.py:311
  85.7 1.6 %copy.21 = bf16[32,2048]{1,0:T(8,128)(2,1)} copy(bf16[32,2048]{1,0:T(8,128)(2,1)} %bitcast.17) | data formatting | bytes 262144

commit v5 on v4

--- a/solution.py
+++ b/solution.py
@@ -13,7 +13,7 @@
 F32 = jnp.float32
 BF16 = jnp.bfloat16
 NT = (((1,), (1,)), ((), ()))
-VMEM_LIMIT = 60 * 1024 * 1024
+VMEM_LIMIT = 107 * 512 * 1024
 
 
 def mm(a, b):
@@ -108,42 +108,47 @@
             c_new[r] = jnp.where(hit, jnp.concatenate([col, col], axis=-1), c_v[r])
         cache_out(g).start()
 
-    for g in range(groups):
-        if g % 2 == 0:
-            cache_in(g).wait()
-            cache_in(g + 1).wait()
-        q16 = qb16[g * 16:(g + 1) * 16, 0:lat + rope]
-        acc = None
-        for i in range(per):
-            s_i = mm(q16, c_v[g * per + i])
-            acc = s_i if acc is None else jnp.where(row_w == i, s_i, acc)
-        sc_s[g * 16:(g + 1) * 16, :] = acc
-        insert(g)
     pairs = rows * heads
-    mine = lax.broadcasted_iota(jnp.int32, (pairs, rows), 0) // heads == lax.broadcasted_iota(jnp.int32, (pairs, rows), 1)
     ent = ent_f[:, 0:rows].astype(BF16)
-    s_new = jnp.sum(jnp.where(mine, mm(qb16[:, 0:lat + rope], ent), 0.0), axis=-1, keepdims=True) * scale
-    len_p = jnp.sum(jnp.where(mine, jnp.broadcast_to(lens_row, (pairs, rows)), 0.0), axis=-1, keepdims=True)
-    lane_p = lax.broadcasted_iota(jnp.int32, (pairs, slots), 1).astype(F32)
-    s = jnp.where(lane_p < len_p, sc_s[...] * scale, -1e30)
-    top = jnp.maximum(jnp.max(s, axis=-1, keepdims=True), s_new)
-    e = jnp.exp(s - top)
-    e_new = jnp.exp(s_new - top)
-    total = jnp.sum(e, axis=-1, keepdims=True) + e_new
-    p_s[...] = jnp.where(lane_p < len_p, e / total, 0.0).astype(BF16)
-    p_new = jnp.where(mine, jnp.broadcast_to(e_new / total, (pairs, rows)), 0.0).astype(BF16)
-    o_new = lax.dot_general(p_new, ent[0:lat], NT, preferred_element_type=F32)
-    for c in range(lat // 128):
-        os[c] = o_new[:, c * 128:(c + 1) * 128]
-
-    for g in range(groups):
-        p16 = p_s[g * 16:(g + 1) * 16, :]
-        acc = None
-        for i in range(per):
-            o_i = lax.dot_general(p16, c_v[g * per + i, 0:lat, :], NT, preferred_element_type=F32)
-            acc = o_i if acc is None else jnp.where(row_l == i, o_i, acc)
+    mine_all = lax.broadcasted_iota(jnp.int32, (pairs, rows), 0) // heads == lax.broadcasted_iota(jnp.int32, (pairs, rows), 1)
+    s_new_all = jnp.sum(jnp.where(mine_all, mm(qb16[:, 0:lat + rope], ent), 0.0), axis=-1, keepdims=True) * scale
+    len_all = jnp.sum(jnp.where(mine_all, jnp.broadcast_to(lens_row, (pairs, rows)), 0.0), axis=-1, keepdims=True)
+    parts = 2
+    span = pairs // parts
+    lane_p = lax.broadcasted_iota(jnp.int32, (span, slots), 1).astype(F32)
+    for t in range(parts):
+        block = range(t * groups // parts, (t + 1) * groups // parts)
+        for g in block:
+            if g % 2 == 0:
+                cache_in(g).wait()
+                cache_in(g + 1).wait()
+            q16 = qb16[g * 16:(g + 1) * 16, 0:lat + rope]
+            acc = None
+            for i in range(per):
+                s_i = mm(q16, c_v[g * per + i])
+                acc = s_i if acc is None else jnp.where(row_w == i, s_i, acc)
+            sc_s[g * 16:(g + 1) * 16, :] = acc
+            insert(g)
+        lo, hi = t * span, (t + 1) * span
+        s_new, len_p, mine = s_new_all[lo:hi], len_all[lo:hi], mine_all[lo:hi]
+        s = jnp.where(lane_p < len_p, sc_s[lo:hi, :] * scale, -1e30)
+        top = jnp.maximum(jnp.max(s, axis=-1, keepdims=True), s_new)
+        e = jnp.exp(s - top)
+        e_new = jnp.exp(s_new - top)
+        total = jnp.sum(e, axis=-1, keepdims=True) + e_new
+        p_s[lo:hi, :] = jnp.where(lane_p < len_p, e / total, 0.0).astype(BF16)
+        p_new = jnp.where(mine, jnp.broadcast_to(e_new / total, (span, rows)), 0.0).astype(BF16)
+        o_new = lax.dot_general(p_new, ent[0:lat], NT, preferred_element_type=F32)
         for c in range(lat // 128):
-            os[c, g * 16:(g + 1) * 16, :] += acc[:, c * 128:(c + 1) * 128]
+            os[c, lo:hi, :] = o_new[:, c * 128:(c + 1) * 128]
+        for g in block:
+            p16 = p_s[g * 16:(g + 1) * 16, :]
+            acc = None
+            for i in range(per):
+                o_i = lax.dot_general(p16, c_v[g * per + i, 0:lat, :], NT, preferred_element_type=F32)
+                acc = o_i if acc is None else jnp.where(row_l == i, o_i, acc)
+            for c in range(lat // 128):
+                os[c, g * 16:(g + 1) * 16, :] += acc[:, c * 128:(c + 1) * 128]
     copies[qa_n + 3].wait()
     for hd in range(heads):
         o_lat = jnp.concatenate([os[c, pl.ds(hd, rows, stride=heads), :].astype(BF16) for c in range(lat // 128)], axis=-1)
@@ -157,7 +162,7 @@
 
 
 def attn_call(layer, x, lengths, attn_gain, kv_gain, q_gain, cache_t, w_dkv_t, w_qa, w_qb, w_uk, w_uv, w_o):
-    any_spec = pl.BlockSpec(memory_space=pl.ANY)
+    hbm = pl.BlockSpec(memory_space=pltpu.HBM)
     vmem = pl.BlockSpec(memory_space=pltpu.VMEM)
     smem = pl.BlockSpec(memory_space=pltpu.SMEM)
     rows, width, slots = cache_t.shape
@@ -165,8 +170,8 @@
     return pl.pallas_call(
         functools.partial(attn_kernel, layer),
         out_shape=(jax.ShapeDtypeStruct(x.shape, F32), jax.ShapeDtypeStruct(cache_t.shape, BF16)),
-        in_specs=[vmem, smem, vmem, vmem, vmem, vmem] + [any_spec] * 7,
-        out_specs=(vmem, any_spec),
+        in_specs=[vmem, smem, vmem, vmem, vmem, vmem] + [hbm] * 7,
+        out_specs=(vmem, hbm),
         scratch_shapes=[
             pltpu.VMEM(cache_t.shape, BF16),
             pltpu.VMEM(cache_t.shape, BF16),
@@ -302,6 +307,7 @@
 
 def ffn_call(layer, n_tp, n_dp, part, x, ffn_gain, w_gate, w_up, w_down):
     any_spec = pl.BlockSpec(memory_space=pl.ANY)
+    hbm = pl.BlockSpec(memory_space=pltpu.HBM)
     vmem = pl.BlockSpec(memory_space=pltpu.VMEM)
     rows, dim = x.shape
     own = rows // n_tp
@@ -311,7 +317,7 @@
     out = pl.pallas_call(
         functools.partial(ffn_kernel, layer, n_tp, n_dp),
         out_shape=jax.ShapeDtypeStruct((n_tp, own, dim), BF16),
-        in_specs=[any_spec] * 6,
+        in_specs=[any_spec] * 3 + [hbm] * 3,
         out_specs=vmem,
         scratch_shapes=[
             pltpu.VMEM((n_tp, own, dim), F32),

time: 87.4 us -> 88.6 us (1.014)
  local copies, waits for them, and re-layouts: 1.57 us -> 5.73 us
  Pallas kernels: 85 us -> 81.8 us
    unnamed x1 -> x25, local copies, waits for them, and re-layouts: 1.57 us -> 5.73 us
    pallas_call x2, Pallas kernels: 28.4 us -> 26.6 us  [attn_call(): pl.pallas_call(functools.partial(attn_kernel, layer), out_shape=(jax.Shap...]
    pallas_call x2, Pallas kernels: 56.6 us -> 55.2 us  [ffn_call(): pl.pallas_call(functools.partial(ffn_kernel, layer, n_tp, n_dp), out_shap...]
where the time goes in v5:
time: 88.6 us; the launch traced here: 88.2 us
  Pallas kernels  81.8 us (92%)
  local copies, waits for them, and re-layouts  5.73 us (6%)
    pallas_call x2, Pallas kernels, ffn_call(): pl.pallas_call(functools.partial(ffn_kernel, layer, n_tp, n_dp), out_shap...  55.2 us
    pallas_call x2, Pallas kernels, attn_call(): pl.pallas_call(functools.partial(attn_kernel, layer), out_shape=(jax.Shap...  26.6 us
    unnamed x25, local copies, waits for them, and re-layouts  5.73 us

profile of v5, /device:TPU:0, one launch (start us, length us, event | category | flops | bytes accessed | tf_op | source)
XLA Modules:
  0.0 88.2 jit_solution(18091209675432546246)
XLA Ops:
  0.6 0.0 copy-start
  0.6 0.9 %copy-done = bf16[32,2048]{1,0:T(8,128)(2,1)S(1)} copy-done((bf16[32,2048]{1,0:T(8,128)(2,1)S(1)}, bf16[32,2048]{1,0:T(8,128)(2,1)}, u32[]{:S(2)}) %copy-start) | copy-done | bytes 131096
  1.5 0.0 copy-start.3
  1.5 0.7 copy-done.3
  2.3 0.0 copy-start.6
  2.3 0.7 copy-done.6
  3.0 0.0 copy-start.8
  3.0 0.7 copy-done.8
  3.6 0.0 copy-start.10
  3.6 0.7 copy-done.10
  4.3 0.0 copy-start.5
  4.3 13.3 %attn0.1 = (f32[32,2048]{1,0:T(8,128)S(1)}, bf16[32,576,256]{2,1,0:T(8,128)(2,1)}) custom-call(bf16[32,2048]{1,0:T(8,128)(2,1)S(1)} %copy-done, s32[32]{0:T(128)S(1)} %copy-done.10, s32[1,32]{1,0:T(1,128)S(1)} %bitcast.16, f32[2,2048]{1,0:T(2,128)S(1)} %copy-done.3, f32[2,512]{1,0:T(2,128)S(1)} %copy-done.8, f32[2,1536]{1,0:T(2,128)S(1)} %copy-done.6, ...), custom_call_target="tpu_custom_call" | custom-call | flops 2000000000 | bytes 33000000 | tf_op jit(solution)/shard_map/attn0/pallas_call | solution.py:170
  17.6 0.0 copy-start.2
  17.6 0.7 copy-done.2
  18.3 0.0 copy-done.5
  18.3 0.0 copy-start.4
  18.3 0.0 copy-start.7
  18.3 0.0 copy-start.9
  18.3 0.0 copy-start.11
  18.3 29.1 %ffn0.1.x = bf16[4,8,2048]{2,1,0:T(8,128)(2,1)S(1)} custom-call(f32[4,8,2048]{2,1,0:T(8,128)} %bitcast.15, bf16[4,8,2048]{2,1,0:T(8,128)(2,1)S(1)} %bitcast.12, f32[2,2048]{1,0:T(2,128)S(1)} %copy-done.5, bf16[2,2048,11264]{2,1,0:T(8,128)(2,1)} %w_gate.3, bf16[2,2048,11264]{2,1,0:T(8,128)(2,1)} %w_up.3, bf16[2,11264,2048]{2,1,0:T(8,128)(2,1)} %w_down.3), custom_call_target="tpu_custom_call" | custom-call | flops 1100000000 | bytes 35000000 | tf_op jit(solution)/shard_map/ffn0/pallas_call | solution.py:317
  47.5 0.0 copy-done.4
  47.5 0.0 copy-done.7
  47.5 0.0 copy-done.9
  47.5 0.0 copy-done.11
  47.5 13.3 %attn1.1 = (f32[32,2048]{1,0:T(8,128)S(1)}, bf16[32,576,256]{2,1,0:T(8,128)(2,1)}) custom-call(bf16[32,2048]{1,0:T(8,128)(2,1)S(1)} %bitcast.11, s32[32]{0:T(128)S(1)} %copy-done.11, s32[1,32]{1,0:T(1,128)S(1)} %bitcast.17, f32[2,2048]{1,0:T(2,128)S(1)} %copy-done.4, f32[2,512]{1,0:T(2,128)S(1)} %copy-done.9, f32[2,1536]{1,0:T(2,128)S(1)} %copy-done.7, ...), custom_call_target="tpu_custom_call" | custom-call | flops 2000000000 | bytes 33000000 | tf_op jit(solution)/shard_map/attn1/pallas_call | solution.py:170
  60.8 0.0 copy-start.1
  60.8 0.7 copy-done.1
  61.5 26.1 %ffn1.1 = bf16[4,8,2048]{2,1,0:T(8,128)(2,1)S(1)} custom-call(f32[4,8,2048]{2,1,0:T(8,128)} %bitcast.14, bf16[4,8,2048]{2,1,0:T(8,128)(2,1)S(1)} %ffn0.1.x, f32[2,2048]{1,0:T(2,128)S(1)} %copy-done.5, bf16[2,2048,11264]{2,1,0:T(8,128)(2,1)} %w_gate.3, bf16[2,2048,11264]{2,1,0:T(8,128)(2,1)} %w_up.3, bf16[2,11264,2048]{2,1,0:T(8,128)(2,1)} %w_down.3), custom_call_target="tpu_custom_call" | custom-call | flops 1100000000 | bytes 35000000 | tf_op jit(solution)/shard_map/ffn1/pallas_call | solution.py:317
  87.6 0.7 copy.21
Async XLA Ops:
  0.6 0.9 %copy-start = (bf16[32,2048]{1,0:T(8,128)(2,1)S(1)}, bf16[32,2048]{1,0:T(8,128)(2,1)}, u32[]{:S(2)}) copy-start(bf16[32,2048]{1,0:T(8,128)(2,1)} %x_ref.1) | copy-start | bytes 393220
  1.5 0.7 copy-start.3
  2.3 0.7 copy-start.6
  3.0 0.7 copy-start.8
  3.6 0.7 copy-start.10
  4.3 14.0 %copy-start.5 = (f32[2,2048]{1,0:T(2,128)S(1)}, f32[2,2048]{1,0:T(2,128)}, u32[]{:S(2)}) copy-start(f32[2,2048]{1,0:T(2,128)} %gain.3) | copy-start | bytes 49156
  17.6 0.7 copy-start.2
  18.3 29.2 %copy-start.4 = (f32[2,2048]{1,0:T(2,128)S(1)}, f32[2,2048]{1,0:T(2,128)}, u32[]{:S(2)}) copy-start(f32[2,2048]{1,0:T(2,128)} %ag_ref.3) | copy-start | bytes 49156
  18.3 29.2 %copy-start.7 = (f32[2,1536]{1,0:T(2,128)S(1)}, f32[2,1536]{1,0:T(2,128)}, u32[]{:S(2)}) copy-start(f32[2,1536]{1,0:T(2,128)} %qg_ref.3) | copy-start | bytes 36868
  18.3 29.2 %copy-start.9 = (f32[2,512]{1,0:T(2,128)S(1)}, f32[2,512]{1,0:T(2,128)}, u32[]{:S(2)}) copy-start(f32[2,512]{1,0:T(2,128)} %kg_ref.3) | copy-start | bytes 12292
  18.3 29.2 %copy-start.11 = (s32[32]{0:T(128)S(1)}, s32[32]{0:T(128)}, u32[]{:S(2)}) copy-start(s32[32]{0:T(128)} %len_s.3) | copy-start | bytes 388
  60.8 0.7 copy-start.1

commit v6 on v5

--- a/solution.py
+++ b/solution.py
@@ -14,6 +14,7 @@
 BF16 = jnp.bfloat16
 NT = (((1,), (1,)), ((), ()))
 VMEM_LIMIT = 107 * 512 * 1024
+FULL_VMEM = 60 * 1024 * 1024
 
 
 def mm(a, b):
@@ -193,7 +194,7 @@
             pltpu.SemaphoreType.DMA((8,)),
             pltpu.SemaphoreType.DMA((8,)),
         ],
-        compiler_params=pltpu.CompilerParams(vmem_limit_bytes=VMEM_LIMIT),
+        compiler_params=pltpu.CompilerParams(vmem_limit_bytes=VMEM_LIMIT if layer else FULL_VMEM),
         cost_estimate=pl.CostEstimate(flops=2_000_000_000, bytes_accessed=33_000_000, transcendentals=0),
         name=f"attn{layer}",
     )(x, lengths, lengths.reshape(1, rows), attn_gain, kv_gain, q_gain, cache_t, w_dkv_t, w_qa, w_qb, w_uk, w_uv, w_o)

time: 88.6 us -> 85.2 us (0.962)
  local copies, waits for them, and re-layouts: 5.73 us -> 1.38 us
  Pallas kernels: 81.8 us -> 82.9 us
    unnamed x25 -> x15, local copies, waits for them, and re-layouts: 5.73 us -> 1.38 us
    pallas_call x2, Pallas kernels: 26.6 us -> 27.7 us  [attn_call(): pl.pallas_call(functools.partial(attn_kernel, layer), out_shape=(jax.Shap...]
where the time goes in v6:
time: 85.2 us; the launch traced here: 85.1 us
  Pallas kernels  82.9 us (97%)
  local copies, waits for them, and re-layouts  1.38 us (2%)
    pallas_call x2, Pallas kernels, ffn_call(): pl.pallas_call(functools.partial(ffn_kernel, layer, n_tp, n_dp), out_shap...  55.2 us
    pallas_call x2, Pallas kernels, attn_call(): pl.pallas_call(functools.partial(attn_kernel, layer), out_shape=(jax.Shap...  27.7 us

profile of v6, /device:TPU:0, one launch (start us, length us, event | category | flops | bytes accessed | tf_op | source)
XLA Modules:
  0.0 85.1 jit_solution(4337976109458362363)
XLA Ops:
  0.6 0.0 copy-start
  0.6 0.0 copy-start.3
  0.6 14.4 %attn0.1 = (f32[32,2048]{1,0:T(8,128)}, bf16[32,576,256]{2,1,0:T(8,128)(2,1)}) custom-call(bf16[32,2048]{1,0:T(8,128)(2,1)} %x_ref.1, s32[32]{0:T(128)} %len_s.3, s32[1,32]{1,0:T(1,128)} %bitcast.15, f32[2,2048]{1,0:T(2,128)} %ag_ref.3, f32[2,512]{1,0:T(2,128)} %kg_ref.3, f32[2,1536]{1,0:T(2,128)} %qg_ref.3, bf16[32,576,256]{2,1,0:T(8,128)(2,1)} %bitcast.19, ...), custom_call_target="tpu_custom_call" | custom-call | flops 2000000000 | bytes 33000000 | tf_op jit(solution)/shard_map/attn0/pallas_call | solution.py:171
  15.1 0.0 copy-done
  15.1 0.0 copy-done.3
  15.1 0.0 copy-start.2
  15.1 0.0 copy-start.4
  15.1 0.0 copy-start.5
  15.2 0.0 copy-start.6
  15.2 29.1 %ffn0.1.x = bf16[4,8,2048]{2,1,0:T(8,128)(2,1)S(1)} custom-call(f32[4,8,2048]{2,1,0:T(8,128)} %bitcast.21, bf16[4,8,2048]{2,1,0:T(8,128)(2,1)S(1)} %bitcast.12, f32[2,2048]{1,0:T(2,128)S(1)} %copy-done.3, bf16[2,2048,11264]{2,1,0:T(8,128)(2,1)} %w_gate.3, bf16[2,2048,11264]{2,1,0:T(8,128)(2,1)} %w_up.3, bf16[2,11264,2048]{2,1,0:T(8,128)(2,1)} %w_down.3), custom_call_target="tpu_custom_call" | custom-call | flops 1100000000 | bytes 35000000 | tf_op jit(solution)/shard_map/ffn0/pallas_call | solution.py:318
  44.3 0.0 copy-done.2
  44.3 0.0 copy-done.4
  44.3 0.0 copy-done.5
  44.3 0.0 copy-done.6
  44.3 13.3 %attn1.1 = (f32[32,2048]{1,0:T(8,128)S(1)}, bf16[32,576,256]{2,1,0:T(8,128)(2,1)}) custom-call(bf16[32,2048]{1,0:T(8,128)(2,1)S(1)} %bitcast.11, s32[32]{0:T(128)S(1)} %copy-done.6, s32[1,32]{1,0:T(1,128)S(1)} %bitcast.16, f32[2,2048]{1,0:T(2,128)S(1)} %copy-done.2, f32[2,512]{1,0:T(2,128)S(1)} %copy-done.5, f32[2,1536]{1,0:T(2,128)S(1)} %copy-done.4, ...), custom_call_target="tpu_custom_call" | custom-call | flops 2000000000 | bytes 33000000 | tf_op jit(solution)/shard_map/attn1/pallas_call | solution.py:171
  57.6 0.0 copy-start.1
  57.7 0.7 copy-done.1
  58.3 26.1 %ffn1.1 = bf16[4,8,2048]{2,1,0:T(8,128)(2,1)S(1)} custom-call(f32[4,8,2048]{2,1,0:T(8,128)} %bitcast.14, bf16[4,8,2048]{2,1,0:T(8,128)(2,1)S(1)} %ffn0.1.x, f32[2,2048]{1,0:T(2,128)S(1)} %copy-done.3, bf16[2,2048,11264]{2,1,0:T(8,128)(2,1)} %w_gate.3, bf16[2,2048,11264]{2,1,0:T(8,128)(2,1)} %w_up.3, bf16[2,11264,2048]{2,1,0:T(8,128)(2,1)} %w_down.3), custom_call_target="tpu_custom_call" | custom-call | flops 1100000000 | bytes 35000000 | tf_op jit(solution)/shard_map/ffn1/pallas_call | solution.py:318
  84.4 0.7 copy.21
Async XLA Ops:
  0.6 14.5 %copy-start = (bf16[32,2048]{1,0:T(8,128)(2,1)S(1)}, bf16[32,2048]{1,0:T(8,128)(2,1)}, u32[]{:S(2)}) copy-start(bf16[32,2048]{1,0:T(8,128)(2,1)} %x_ref.1) | copy-start | bytes 393220
  0.6 14.5 %copy-start.3 = (f32[2,2048]{1,0:T(2,128)S(1)}, f32[2,2048]{1,0:T(2,128)}, u32[]{:S(2)}) copy-start(f32[2,2048]{1,0:T(2,128)} %gain.3) | copy-start | bytes 49156
  15.1 29.2 %copy-start.2 = (f32[2,2048]{1,0:T(2,128)S(1)}, f32[2,2048]{1,0:T(2,128)}, u32[]{:S(2)}) copy-start(f32[2,2048]{1,0:T(2,128)} %ag_ref.3) | copy-start | bytes 49156
  15.1 29.2 %copy-start.4 = (f32[2,1536]{1,0:T(2,128)S(1)}, f32[2,1536]{1,0:T(2,128)}, u32[]{:S(2)}) copy-start(f32[2,1536]{1,0:T(2,128)} %qg_ref.3) | copy-start | bytes 36868
  15.1 29.2 %copy-start.5 = (f32[2,512]{1,0:T(2,128)S(1)}, f32[2,512]{1,0:T(2,128)}, u32[]{:S(2)}) copy-start(f32[2,512]{1,0:T(2,128)} %kg_ref.3) | copy-start | bytes 12292
  15.2 29.2 %copy-start.6 = (s32[32]{0:T(128)S(1)}, s32[32]{0:T(128)}, u32[]{:S(2)}) copy-start(s32[32]{0:T(128)} %len_s.3) | copy-start | bytes 388
  57.6 0.7 copy-start.1
